TPU v7x, 32 devices: a whole 2x2x4 slice. The times are simulated.
32 devices in a mesh: dp: 8 (over z, y), mp: 4 (over x, core).
Axes of the slice: x: 2, y: 2, z: 4, core: 2. Of those that a mesh axis runs over, the one named last changes fastest.
Arguments:
- inputs: bfloat16 [8192, 768], P(('dp', 'mp')), may hold values from -6 to 6
- memory: bfloat16 [32768, 768], P(('dp', 'mp')), may hold values from -6 to 6
- target_len: int32 [64], P('dp'), may hold values from 8 to 114, as said below
- memory_len: int32 [64], P('dp'), may hold values from 32 to 512, as said below
- bucket_map: int32 [128], replicated, may hold values from 0 to 31, as said below
- self_gain: float32 [768], replicated, may hold values from 0.5 to 1.5
- self_query: bfloat16 [768, 768], P(None, 'mp'), may hold values from -0.02734375 to 0.02734375
- self_key: bfloat16 [768, 768], P(None, 'mp'), may hold values from -0.21875 to 0.21875
- self_value: bfloat16 [768, 768], P(None, 'mp'), may hold values from -0.21875 to 0.21875
- self_out: bfloat16 [768, 768], P('mp'), may hold values from -1.25 to 1.25
- bias_table: float32 [32, 12], P(None, 'mp'), may hold values from -4 to 4
- cross_gain: float32 [768], replicated, may hold values from 0.5 to 1.5
- cross_query: bfloat16 [768, 768], P(None, 'mp'), may hold values from -0.02734375 to 0.02734375
- cross_key: bfloat16 [768, 768], P(None, 'mp'), may hold values from -0.21875 to 0.21875
- cross_value: bfloat16 [768, 768], P(None, 'mp'), may hold values from -0.21875 to 0.21875
- cross_out: bfloat16 [768, 768], P('mp'), may hold values from -2.5 to 2.5
- feed_gain: float32 [768], replicated, may hold values from 0.5 to 1.5
- feed_input: bfloat16 [768, 3072], P(None, 'mp'), may hold values from -0.21875 to 0.21875
- feed_output: bfloat16 [3072, 768], P('mp'), may hold values from -0.15625 to 0.15625
- cotangent: bfloat16 [8192, 768], P(('dp', 'mp')), may hold values from -6 to 6
Outputs:
- layer_out: bfloat16 [8192, 768], P(('dp', 'mp'))
- inputs_grad: float32 [8192, 768], P(('dp', 'mp'))
- memory_grad: float32 [32768, 768], P(('dp', 'mp'))
- self_gain_grad: float32 [768], replicated
- self_query_grad: float32 [768, 768], P(None, 'mp')
- self_key_grad: float32 [768, 768], P(None, 'mp')
- self_value_grad: float32 [768, 768], P(None, 'mp')
- self_out_grad: float32 [768, 768], P('mp')
- bias_table_grad: float32 [32, 12], P(None, 'mp')
- cross_gain_grad: float32 [768], replicated
- cross_query_grad: float32 [768, 768], P(None, 'mp')
- cross_key_grad: float32 [768, 768], P(None, 'mp')
- cross_value_grad: float32 [768, 768], P(None, 'mp')
- cross_out_grad: float32 [768, 768], P('mp')
- feed_gain_grad: float32 [768], replicated
- feed_input_grad: float32 [768, 3072], P(None, 'mp')
- feed_output_grad: float32 [3072, 768], P('mp')
Inputs may be any that keep to these rules, and one draw needn't show every extreme that they name: bucket_map[d] is the bucket of a key d positions before its query: it equals d below 16, never falls as d grows, and reaches 31. An example's target rows at positions from target_len on are padding. An example's memory rows at positions from memory_len on are padding.
All inputs are finite; a program needn't handle non-finite values.
Results may differ from a plain program's by a relative error of at most 0.023.
Values may be sent and summed in bfloat16 or wider, within the bound.
No kernel may reach another device: no remote copies, remote signals or barrier semaphores. Data moves between devices by JAX's collectives and lax.ppermute only.
A program may use at most 128 MiB of HBM per device.

v0:
```python
import functools

import jax
import jax.numpy as jnp
from jax import lax
from jax.experimental import pallas as pl
from jax.experimental.pallas import tpu as pltpu
from jax.sharding import PartitionSpec as P

HEAD_DIM = 64
PAIR = 2 * HEAD_DIM
BUCKETS = 32
TGT_LEN = 128
MEM_LEN = 512

masked_fill = -1000000000.0
epsilon = 1e-06
highest = lax.Precision.HIGHEST
tanh_scale = 0.7978845608
cubic_term = 0.044715
bf16 = jnp.bfloat16
f32 = jnp.float32


def dot_nn(a, b):
    return lax.dot_general(a, b, (((1,), (0,)), ((), ())), preferred_element_type=f32)


def dot_nt(a, b):
    return lax.dot_general(a, b, (((1,), (1,)), ((), ())), preferred_element_type=f32)


def dot_tn(a, b):
    return lax.dot_general(a, b, (((0,), (0,)), ((), ())), preferred_element_type=f32)


def row_scale(hidden):
    return lax.rsqrt(jnp.mean(hidden * hidden, -1, keepdims=True) + epsilon)


def norm_backward(hidden, scale, gain, upstream):
    weighted = gain * upstream
    return scale * weighted - hidden * (scale * scale * scale) * jnp.mean(hidden * weighted, -1, keepdims=True)


def matrix(blocks, index, width):
    return jnp.concatenate([b[index * width : (index + 1) * width, :] for b in blocks], 0)


def store_rows(ref, lead, index, grad, turn):
    blocks = ref.shape[len(lead)]
    size = grad.shape[0] // blocks
    for a in range(blocks):
        ref[(*lead, a ^ turn, index)] = grad[a * size : (a + 1) * size].astype(bf16)


def store_grad(keep_ref, send_ref, index, grad, turn):
    width = grad.shape[0] // 4
    for j in range(4):
        store_rows((keep_ref, send_ref)[j % 2], (j // 2,), index, grad[j * width : (j + 1) * width], turn)


def pair_masks():
    lane = lax.broadcasted_iota(jnp.int32, (1, PAIR), 1)
    return (lane < HEAD_DIM).astype(bf16), (lane >= HEAD_DIM).astype(bf16)


def stack_pair(rows, masks):
    return jnp.concatenate([rows * masks[0], rows * masks[1]], 0)


def unstack_pair(both):
    lane = lax.broadcasted_iota(jnp.int32, (TGT_LEN, PAIR), 1)
    return jnp.where(lane < HEAD_DIM, both[:TGT_LEN], both[TGT_LEN:])


def softmax_rows(scores):
    weights = jnp.exp(scores - jnp.max(scores, -1, keepdims=True))
    return weights * (1.0 / jnp.sum(weights, -1, keepdims=True))


def locate(step, pairs, keys):
    example = lax.div(step, pairs)
    pair = lax.rem(step, pairs)
    rows = pl.ds(pl.multiple_of(example * TGT_LEN, TGT_LEN), TGT_LEN)
    key_rows = pl.ds(pl.multiple_of(example * keys, keys), keys)
    cols = pl.ds(pl.multiple_of(pair * PAIR, PAIR), PAIR)
    return example, pair, rows, key_rows, cols


def cross_probs(queries, key_rows, length):
    scores = dot_nt(queries, key_rows)
    key = lax.broadcasted_iota(jnp.int32, scores.shape, 1)
    return softmax_rows(jnp.where(key < length, scores, masked_fill))


def attend(q_ref, k_ref, v_ref, mixed_ref, keys, probs_of):
    masks = pair_masks()
    pairs = q_ref.shape[1] // PAIR
    examples = q_ref.shape[0] // TGT_LEN

    def step(i, carry):
        example, pair, rows, key_rows, cols = locate(i, pairs, keys)
        probs = probs_of(stack_pair(q_ref[rows, cols], masks), k_ref[key_rows, cols], example, pair)
        mixed = dot_nn(probs.astype(bf16), v_ref[key_rows, cols])
        mixed_ref[rows, cols] = unstack_pair(mixed).astype(bf16)
        return carry

    lax.fori_loop(0, examples * pairs, step, 0, unroll=2)


def attend_back(q_ref, k_ref, v_ref, m_ref, dq_ref, dk_ref, dv_ref, keys, probs_of):
    masks = pair_masks()
    pairs = q_ref.shape[1] // PAIR
    examples = q_ref.shape[0] // TGT_LEN

    def step(i, carry):
        example, pair, rows, key_rows, cols = locate(i, pairs, keys)
        queries = stack_pair(q_ref[rows, cols], masks)
        grads = stack_pair(m_ref[rows, cols], masks)
        key_block = k_ref[key_rows, cols]
        probs = probs_of(queries, key_block, example, pair)
        dv_ref[key_rows, cols] = dot_tn(probs.astype(bf16), grads).astype(bf16)
        prob_grad = dot_nt(grads, v_ref[key_rows, cols])
        score_grad = probs * (prob_grad - jnp.sum(probs * prob_grad, -1, keepdims=True))
        low = score_grad.astype(bf16)
        dq_ref[rows, cols] = unstack_pair(dot_nn(low, key_block)).astype(bf16)
        dk_ref[key_rows, cols] = dot_tn(low, queries).astype(bf16)
        return carry

    lax.fori_loop(0, examples * pairs, step, 0, unroll=UNROLL_BACK)


UNROLL_BACK = 2


def fill_bias(table_ref, bias_ref):
    for head in range(bias_ref.shape[0] // TGT_LEN):
        row = jnp.broadcast_to(table_ref[head : head + 1, :], (TGT_LEN, TGT_LEN))
        bias_ref[head * TGT_LEN : (head + 1) * TGT_LEN, :] = pltpu.roll(row, 0, axis=1, stride=1, stride_axis=0)


def stack_heads(rows):
    lane = lax.broadcasted_iota(jnp.int32, (1, rows.shape[1]), 1)
    heads = rows.shape[1] // HEAD_DIM
    return jnp.concatenate([rows * (lax.div(lane, HEAD_DIM) == h).astype(bf16) for h in range(heads)], 0)


def unstack_heads(stacked):
    length = TGT_LEN
    lane = lax.broadcasted_iota(jnp.int32, (length, stacked.shape[1]), 1)
    out = stacked[:length]
    for h in range(1, stacked.shape[1] // HEAD_DIM):
        out = jnp.where(lane >= h * HEAD_DIM, stacked[h * length : (h + 1) * length], out)
    return out


def self_probs(queries, key_rows, bias, length):
    scores = dot_nt(queries, key_rows) + bias
    key = lax.broadcasted_iota(jnp.int32, scores.shape, 1)
    query = lax.rem(lax.broadcasted_iota(jnp.int32, scores.shape, 0), TGT_LEN)
    return softmax_rows(jnp.where((key <= query) & (key < length), scores, masked_fill))


def diagonal_sums(grad):
    query = lax.broadcasted_iota(jnp.int32, grad.shape, 0)
    for bit in range(TGT_LEN.bit_length() - 1):
        moved = pltpu.roll(grad, TGT_LEN - (1 << bit), axis=1)
        grad = jnp.where((query >> bit) & 1 == 1, moved, grad)
    return jnp.sum(grad, 0, keepdims=True)


def first_norm(x_ref, gain_ref, n_ref):
    hidden = x_ref[...].astype(f32)
    n_ref[...] = (hidden * row_scale(hidden) * gain_ref[...]).astype(bf16)


def store_parts(own_ref, chip_ref, send_ref, parts):
    for j, part in enumerate(parts):
        if j == 0:
            own_ref[...] = part
        elif j == 2:
            chip_ref[...] = part
        else:
            send_ref[j // 2] = part.astype(bf16)


def self_forward(
    n0, n1, n2, n3, wq_ref, wk_ref, wv_ref, wo_ref, table_ref, rank_ref, len_ref,
    q_ref, k_ref, v_ref, mixed_ref, own_ref, chip_ref, send_ref, bias_ref,
):
    fill_bias(table_ref, bias_ref)
    size = n0.shape[0]
    for j, n in enumerate((n0, n1, n2, n3)):
        rows = slice(j * size, (j + 1) * size)
        for ref, w in ((q_ref, wq_ref), (k_ref, wk_ref), (v_ref, wv_ref)):
            ref[rows, :] = dot_nn(n[...], w[...]).astype(bf16)

    def step(i, carry):
        rows = pl.ds(pl.multiple_of(i * TGT_LEN, TGT_LEN), TGT_LEN)
        length = len_ref[(rank_ref[0] * (size // TGT_LEN)) ^ i]
        probs = self_probs(stack_heads(q_ref[rows, :]), k_ref[rows, :], bias_ref[...], length)
        mixed_ref[rows, :] = unstack_heads(dot_nn(probs.astype(bf16), v_ref[rows, :])).astype(bf16)
        return carry

    lax.fori_loop(0, 4 * size // TGT_LEN, step, 0, unroll=2)
    store_parts(
        own_ref, chip_ref, send_ref,
        (dot_nn(mixed_ref[j * size : (j + 1) * size, :], wo_ref[...]) for j in range(4)),
    )


def memory_forward(mem_ref, w0, w1, w2, w3, k_ref, v_ref):
    width = k_ref.shape[1] // 4
    blocks = (w0, w1, w2, w3)
    k_ref[...] = dot_nt(mem_ref[...], matrix(blocks, 0, width)).astype(bf16)
    v_ref[...] = dot_nt(mem_ref[...], matrix(blocks, 1, width)).astype(bf16)


def cross_forward(
    x_ref, near_ref, far_ref, k_ref, v_ref, gain_two_ref, gain_three_ref, w0, w1, w2, w3, len_ref,
    after_self_ref, n2_ref, q_ref, mixed_ref, after_ref, n3_ref,
):
    blocks = (w0, w1, w2, w3)
    width = q_ref.shape[1] // 4
    after_self = x_ref[...].astype(f32) + near_ref[...] + far_ref[...].astype(f32)
    after_self_ref[...] = after_self
    normed = (after_self * row_scale(after_self) * gain_two_ref[...]).astype(bf16)
    n2_ref[...] = normed
    q_ref[...] = dot_nt(normed, matrix(blocks, 0, width)).astype(bf16)

    def probs(queries, key_rows, example, pair):
        return cross_probs(queries, key_rows, len_ref[example])

    attend(q_ref, k_ref, v_ref, mixed_ref, MEM_LEN, probs)
    after = after_self_ref[...] + dot_nn(mixed_ref[...], matrix(blocks, 1, width))
    after_ref[...] = after
    n3_ref[...] = (after * row_scale(after) * gain_three_ref[...]).astype(bf16)


def feed_main(
    g0, g1, g2, g3, c0, c1, c2, c3, in_ref, out_ref, own_ref, chip_ref, send_ref, act_ref, pre_grad_ref
):
    for j, (g, c) in enumerate(zip((g0, g1, g2, g3), (c0, c1, c2, c3))):
        rows = slice(j * g.shape[0], (j + 1) * g.shape[0])
        pre = dot_nn(g[...], in_ref[...])
        hidden_grad = dot_nt(c[...], out_ref[...])
        square = pre * pre
        tanh = jnp.tanh(tanh_scale * (pre + cubic_term * square * pre))
        act_ref[rows, :] = (0.5 * pre * (1.0 + tanh)).astype(bf16)
        slope = 0.5 * (1.0 + tanh) + 0.5 * pre * (1.0 - tanh * tanh) * (
            tanh_scale * (1.0 + 3.0 * cubic_term * square)
        )
        low = (hidden_grad * slope).astype(bf16)
        pre_grad_ref[rows, :] = low
        grad = dot_nt(low, in_ref[...])
        if j == 0:
            own_ref[...] = grad
        elif j == 2:
            chip_ref[...] = grad
        else:
            send_ref[j // 2] = grad.astype(bf16)


def feed_rest(
    g0, g1, g2, g3, c0, c1, c2, c3, act_ref, pre_grad_ref, out_ref, turn_ref, own_ref, chip_ref, send_ref, grads_ref
):
    gathered = jnp.concatenate([g[...] for g in (g0, g1, g2, g3)], 0)
    store_rows(grads_ref, (), 0, dot_tn(gathered, pre_grad_ref[...]), turn_ref[0])
    upstream = jnp.concatenate([c[...] for c in (c0, c1, c2, c3)], 0)
    store_rows(grads_ref, (), 1, dot_tn(act_ref[...], upstream), turn_ref[0])
    for j in range(4):
        rows = slice(j * g0.shape[0], (j + 1) * g0.shape[0])
        part = dot_nn(act_ref[rows, :], out_ref[...])
        if j == 0:
            own_ref[...] = part
        elif j == 2:
            chip_ref[...] = part
        else:
            send_ref[j // 2] = part.astype(bf16)


def cross_backward(
    near_ref, far_ref, cot_ref, after_ref, after_self_ref, gain_two_ref, gain_three_ref,
    n2_ref, q_ref, k_ref, v_ref, mixed_ref, w0, w1, w2, w3, len_ref, turn_ref,
    grad_one_ref, up_ref, dk_ref, dv_ref, gains_ref, keep_ref, send_ref, m_ref, dq_ref,
):
    blocks = (w0, w1, w2, w3)
    width = q_ref.shape[1] // 4
    after = after_ref[...]
    scale = row_scale(after)
    upstream = near_ref[...] + far_ref[...].astype(f32)
    gains_ref[1:2, :] = jnp.sum(upstream * after * scale, 0, keepdims=True)
    grad_two = cot_ref[...].astype(f32) + norm_backward(after, scale, gain_three_ref[...], upstream)
    grad_one_ref[...] = grad_two
    up_two = grad_two.astype(bf16)
    m_ref[...] = dot_nt(up_two, matrix(blocks, 1, width)).astype(bf16)
    store_grad(keep_ref, send_ref, 1, dot_tn(mixed_ref[...], up_two), turn_ref[0])

    def probs(queries, key_rows, example, pair):
        return cross_probs(queries, key_rows, len_ref[example])

    attend_back(q_ref, k_ref, v_ref, m_ref, dq_ref, dk_ref, dv_ref, MEM_LEN, probs)
    store_grad(keep_ref, send_ref, 0, dot_tn(dq_ref[...], n2_ref[...]), turn_ref[0])
    upstream = dot_nn(dq_ref[...], matrix(blocks, 0, width))
    hidden = after_self_ref[...]
    scale = row_scale(hidden)
    gains_ref[0:1, :] = jnp.sum(upstream * hidden * scale, 0, keepdims=True)
    grad_one = grad_one_ref[...] + norm_backward(hidden, scale, gain_two_ref[...], upstream)
    grad_one_ref[...] = grad_one
    up_ref[...] = grad_one.astype(bf16)


def memory_weights(dk_ref, dv_ref, mem_ref, keep_in, send_in, turn_ref, keep_ref, send_ref):
    count = keep_in.shape[2]
    for j in range(2):
        for a in range(keep_in.shape[1]):
            keep_ref[j, a, :count] = keep_in[j, a]
            send_ref[j, a, :count] = send_in[j, a]
    store_grad(keep_ref, send_ref, count, dot_tn(dk_ref[...], mem_ref[...]), turn_ref[0])
    store_grad(keep_ref, send_ref, count + 1, dot_tn(dv_ref[...], mem_ref[...]), turn_ref[0])


def self_backward(
    u0, u1, u2, u3, n0, n1, n2, n3, q_ref, k_ref, v_ref, mixed_ref, wq_ref, wk_ref, wv_ref, wo_ref,
    table_ref, rank_ref, len_ref, turn_ref,
    grads_ref, sums_ref, own_ref, chip_ref, send_ref, bias_ref, score_ref, m_ref, dq_ref, dk_ref, dv_ref,
):
    fill_bias(table_ref, bias_ref)
    score_ref[...] = jnp.zeros_like(score_ref)
    size = n0.shape[0]
    width = q_ref.shape[1]
    for j, u in enumerate((u0, u1, u2, u3)):
        m_ref[j * size : (j + 1) * size, :] = dot_nt(u[...], wo_ref[...]).astype(bf16)

    def step(i, carry):
        rows = pl.ds(pl.multiple_of(i * TGT_LEN, TGT_LEN), TGT_LEN)
        length = len_ref[(rank_ref[0] * (size // TGT_LEN)) ^ i]
        queries = stack_heads(q_ref[rows, :])
        grads = stack_heads(m_ref[rows, :])
        key_block = k_ref[rows, :]
        probs = self_probs(queries, key_block, bias_ref[...], length)
        dv_ref[rows, :] = dot_tn(probs.astype(bf16), grads).astype(bf16)
        prob_grad = dot_nt(grads, v_ref[rows, :])
        score_grad = probs * (prob_grad - jnp.sum(probs * prob_grad, -1, keepdims=True))
        score_ref[...] += score_grad
        low = score_grad.astype(bf16)
        dq_ref[rows, :] = unstack_heads(dot_nn(low, key_block)).astype(bf16)
        dk_ref[rows, :] = dot_tn(low, queries).astype(bf16)
        return carry

    lax.fori_loop(0, 4 * size // TGT_LEN, step, 0, unroll=UNROLL_BACK)
    normed = jnp.concatenate([n[...] for n in (n0, n1, n2, n3)], 0)
    upstream = jnp.concatenate([u[...] for u in (u0, u1, u2, u3)], 0)
    for index, (left, right) in enumerate(
        ((dq_ref[...], normed), (dk_ref[...], normed), (dv_ref[...], normed), (mixed_ref[...], upstream))
    ):
        store_rows(grads_ref, (), index, dot_tn(left, right), turn_ref[0])
    heads = width // HEAD_DIM
    sums = [diagonal_sums(score_ref[h * TGT_LEN : (h + 1) * TGT_LEN, :]) for h in range(heads)]
    sums_ref[:heads, :] = jnp.concatenate(sums, 0)
    sums_ref[heads:, :] = jnp.zeros((sums_ref.shape[0] - heads, TGT_LEN), f32)

    def part(j):
        rows = slice(j * size, (j + 1) * size)
        out = dot_nt(dq_ref[rows, :], wq_ref[...])
        return out + dot_nt(dk_ref[rows, :], wk_ref[...]) + dot_nt(dv_ref[rows, :], wv_ref[...])

    store_parts(own_ref, chip_ref, send_ref, (part(j) for j in range(4)))


def last_norm(grad_one_ref, near_ref, far_ref, x_ref, gain_ref, late_ref, sums_ref, rank_ref, grad_ref, small_ref):
    upstream = near_ref[...] + far_ref[...].astype(f32)
    hidden = x_ref[...].astype(f32)
    scale = row_scale(hidden)
    small_ref[...] = jnp.zeros_like(small_ref)
    small_ref[0:1, :] = jnp.sum(upstream * hidden * scale, 0, keepdims=True)
    small_ref[1:3, :] = late_ref[...]
    for j in range(4):
        here = (rank_ref[0] == j).astype(f32)
        small_ref[8 * (j + 1) : 8 * (j + 2), :TGT_LEN] = sums_ref[...] * here
    grad_ref[...] = grad_one_ref[...] + norm_backward(hidden, scale, gain_ref[...], upstream)


def gather_rows(ref, index, turn):
    return jnp.concatenate([ref[a ^ turn, index].astype(f32) for a in range(ref.shape[0])], 0)


def finish_feed(total_ref, turn_ref, in_ref, out_ref):
    in_ref[...] = gather_rows(total_ref, 0, turn_ref[0])
    out_ref[...] = gather_rows(total_ref, 1, turn_ref[0])


def finish_heads(total_ref, turn_ref, *outs):
    for index, ref in enumerate(outs):
        rows = gather_rows(total_ref, index, turn_ref[0])
        ref[...] = rows if ref.shape == rows.shape else rows.T


def memory_backward(dk_ref, dv_ref, w0, w1, w2, w3, grad_ref):
    blocks = (w0, w1, w2, w3)
    width = dk_ref.shape[1] // 4
    grad_ref[...] = dot_nn(dk_ref[...], matrix(blocks, 0, width)) + dot_nn(dv_ref[...], matrix(blocks, 1, width))


def call(kernel, operands, outs, scratch=(), flops=0, smem=()):
    moved = sum(a.size * a.dtype.itemsize for a in operands)
    moved += sum(functools.reduce(lambda x, y: x * y, s) * jnp.dtype(t).itemsize for s, t in outs)
    return pl.pallas_call(
        kernel,
        out_shape=[jax.ShapeDtypeStruct(s, t) for s, t in outs],
        in_specs=[
            pl.BlockSpec(memory_space=pltpu.SMEM if i in smem else pltpu.VMEM) for i in range(len(operands))
        ],
        out_specs=[pl.BlockSpec(memory_space=pltpu.VMEM) for _ in outs],
        scratch_shapes=[pltpu.VMEM(s, t) for s, t in scratch],
        compiler_params=pltpu.CompilerParams(vmem_limit_bytes=VMEM_LIMIT),
        cost_estimate=pl.CostEstimate(flops=flops, bytes_accessed=moved, transcendentals=0),
    )(*operands)


VMEM_LIMIT = 56 * 1024 * 1024


def after(value, *others):
    return lax.optimization_barrier((value, *others))[0]


def swap_core(a):
    return lax.ppermute(a, "mp", [(0, 1), (1, 0), (2, 3), (3, 2)])


def swap_chip(a):
    return lax.ppermute(a, "mp", [(0, 2), (2, 0), (1, 3), (3, 1)])


def gather_blocks(a):
    far = swap_chip(a)
    return (a, swap_core(a), far, swap_core(far))


def core_sum(own, chip, send):
    got = swap_core(send)
    return own.astype(f32) + got[0].astype(f32), (chip.astype(f32) + got[1].astype(f32)).astype(bf16)


def dp_chain(value):
    size = lax.axis_size("dp")
    bits = range(size.bit_length() - 1)
    keep, send = value[: size // 2], value[size // 2 :]
    for bit in bits:
        pairs = [(i, i ^ (1 << bit)) for i in range(size)]
        got = lax.ppermute(send, "dp", pairs)
        token = yield send
        got = after(got, token)
        half = keep.shape[0] // 2
        if half:
            send = (keep[half:].astype(f32) + got[half:].astype(f32)).astype(bf16)
            keep = (keep[:half].astype(f32) + got[:half].astype(f32)).astype(bf16)
        else:
            value = (keep.astype(f32) + got.astype(f32)).astype(bf16)
    for bit in reversed(bits):
        pairs = [(i, i ^ (1 << bit)) for i in range(size)]
        other = lax.ppermute(value, "dp", pairs)
        token = yield value
        value = jnp.concatenate([value, after(other, token)], 0)
    yield value


def sum_all(value):
    steps = [("mp", 1), ("mp", 2)] + [("dp", 1 << bit) for bit in range(lax.axis_size("dp").bit_length() - 1)]
    for axis, flip in steps:
        pairs = [(i, i ^ flip) for i in range(lax.axis_size(axis))]
        got = lax.ppermute(value, axis, pairs)
        token = yield value
        value = value + after(got, token)
    yield value


def next_step(chain, token, first=False):
    try:
        return next(chain) if first else chain.send(token)
    except StopIteration:
        return None


def body(
    inputs,
    memory,
    target_len,
    memory_len,
    bucket_map,
    self_gain,
    self_query,
    self_key,
    self_value,
    self_out,
    bias_table,
    cross_gain,
    cross_query,
    cross_key,
    cross_value,
    cross_out,
    feed_gain,
    feed_input,
    feed_output,
    cotangent,
):
    rank = lax.axis_index("mp")
    rows, d = inputs.shape
    key_rows = memory.shape[0]
    width = self_query.shape[1]
    wide = 4 * width
    heads = bias_table.shape[1]
    units = feed_input.shape[1]
    examples = rows // TGT_LEN
    rank_value = rank.astype(jnp.int32).reshape(1)
    blocks = lax.axis_size("dp")
    place = lax.axis_index("dp").astype(jnp.int32)
    turn = jnp.zeros((1,), jnp.int32)
    for bit in range(blocks.bit_length() - 1):
        turn = 2 * turn + ((place >> bit) & 1)
    memory_len = lax.dynamic_slice_in_dim(memory_len, rank * examples, examples, 0)
    gain_one, gain_two, gain_three = self_gain[None], cross_gain[None], feed_gain[None]

    distance = (TGT_LEN - jnp.arange(TGT_LEN, dtype=jnp.int32)) % TGT_LEN
    lookup = distance[:, None] == jnp.arange(TGT_LEN, dtype=jnp.int32)[None, :]
    bucket = jnp.sum(jnp.where(lookup, bucket_map[None, :], 0), -1)
    hot = (bucket[:, None] == jnp.arange(BUCKETS, dtype=jnp.int32)[None, :]).astype(f32)
    by_distance = lax.dot_general(bias_table, hot, (((0,), (1,)), ((), ())), precision=highest)
    big = (rows, d)
    head_rows = (rows, wide)
    key_heads = (key_rows, wide)
    square = ((heads * TGT_LEN, TGT_LEN), f32)
    group_heads = (4 * rows, width)
    pack = ((2, rows, d), bf16)
    product = 2 * rows * d * wide

    def grad_rows(count, size, lead=()):
        return ((*lead, blocks, count, size // blocks, d), bf16)

    second_own = jnp.concatenate([cross_key.T, cross_value.T], 0)
    third_own = jnp.concatenate([cross_query.T, cross_out], 0)
    normed_one = call(first_norm, (inputs, gain_one), [(big, bf16)])[0]
    ones = gather_blocks(normed_one)
    second_far = swap_chip(after(second_own, ones[2]))
    self_q, self_k, self_v, self_mixed, near, chip, send = call(
        self_forward,
        (*ones, self_query, self_key, self_value, self_out, by_distance, rank_value, target_len),
        [(group_heads, bf16)] * 4 + [(big, f32), (big, f32), pack],
        [square],
        flops=4 * product,
        smem=(9, 10),
    )
    second_far = after(second_far, self_mixed)
    third_far = swap_chip(after(third_own, second_far))
    near, far_send = core_sum(near, chip, send)
    far = swap_chip(far_send)
    second = (second_own, swap_core(second_own), second_far, swap_core(second_far))
    cross_k, cross_v = call(
        memory_forward, (after(memory, far_send), *second), [(key_heads, bf16)] * 2, flops=8 * product
    )
    third_far = after(third_far, cross_v)
    third = (third_own, swap_core(third_own), third_far, swap_core(third_far))
    far = after(far, third_far)
    ups_far = swap_chip(after(cotangent, far))
    after_self, normed_two, cross_q, cross_mixed, after_cross, normed_three = call(
        cross_forward,
        (inputs, near, far, cross_k, cross_v, gain_two, gain_three, *third, memory_len),
        [(big, f32), (big, bf16), (head_rows, bf16), (head_rows, bf16), (big, f32), (big, bf16)],
        flops=6 * product,
        smem=(11,),
    )
    ups_far = after(ups_far, normed_three)
    ups = (cotangent, swap_core(cotangent), ups_far, swap_core(ups_far))
    gathered = gather_blocks(normed_three)
    many = 4 * rows
    near, chip, send, activated, pre_grad = call(
        feed_main,
        (*gathered, *ups, feed_input, feed_output),
        [(big, f32), (big, f32), pack, ((many, units), bf16), ((many, units), bf16)],
        flops=12 * product,
    )
    near, far_send = core_sum(near, chip, send)
    far = swap_chip(far_send)
    out_near, out_chip, out_send, feed_part = call(
        feed_rest,
        (*gathered, *ups, after(activated, far_send), pre_grad, feed_output, turn),
        [(big, f32), (big, f32), pack, grad_rows(2, d)],
        flops=12 * product,
        smem=(11,),
    )
    zero = dp_chain(feed_part)
    token = next(zero)
    far = after(far, token)
    grad_one, up_one, key_grad, value_grad, late_gains, keep, send = call(
        cross_backward,
        (near, far, cotangent, after_cross, after_self, gain_two, gain_three)
        + (normed_two, cross_q, cross_k, cross_v, cross_mixed, *third, memory_len, turn),
        [(big, f32), (big, bf16), (key_heads, bf16), (key_heads, bf16), ((2, d), f32)] + [grad_rows(2, width, (2,))] * 2,
        [(head_rows, bf16), (head_rows, bf16)],
        flops=16 * product,
        smem=(16, 17),
    )
    up_far = swap_chip(up_one)
    keep, send = call(
        memory_weights,
        (key_grad, value_grad, memory, keep, send, turn),
        [grad_rows(4, width, (2,))] * 2,
        flops=8 * product,
        smem=(5,),
    )
    up_far = after(up_far, keep)
    token = zero.send(up_far)
    one_near, one_send = core_sum(keep[0], keep[1], after(send, token))
    one_far = swap_chip(one_send)
    self_ups = (up_one, swap_core(up_one), after(up_far, one_send), swap_core(up_far))
    grads, sums, near, chip, send = call(
        self_backward,
        (*self_ups, *ones, self_q, self_k, self_v, self_mixed)
        + (self_query, self_key, self_value, self_out, by_distance, rank_value, target_len, turn),
        [grad_rows(4, width), ((8, TGT_LEN), f32), (big, f32), (big, f32), pack],
        [square, square] + [(group_heads, bf16)] * 4,
        flops=10 * product,
        smem=(17, 18, 19),
    )
    token = zero.send(sums)
    two = dp_chain(after(grads, token))
    two_token = next(two)
    near, far_send = core_sum(near, chip, after(send, two_token))
    far = swap_chip(far_send)
    memory_grad = call(
        memory_backward,
        (after(key_grad, far_send), value_grad, *second),
        [((key_rows, d), f32)],
        flops=8 * product,
    )[0]
    token = zero.send(memory_grad)
    one = dp_chain((one_near + after(one_far, token).astype(f32)).astype(bf16))
    token = next(one)
    token = two.send(token)
    inputs_grad, small = call(
        last_norm,
        (grad_one, near, after(far, token), inputs, gain_one, late_gains, sums, rank_value),
        [(big, f32), ((40, d), f32)],
        smem=(7,),
    )
    small = sum_all(small)
    token = next_step(small, inputs_grad, True)
    out_near, out_send = core_sum(out_near, out_chip, after(out_send, token))
    out_far = swap_chip(out_send)
    total = {}
    waiting = [(zero, "zero"), (one, "one"), (two, "two"), (small, "small")]
    while waiting:
        still = []
        for chain, name in waiting:
            step = next_step(chain, token)
            if step is None:
                continue
            token = total[name] = step
            still.append((chain, name))
        waiting = still
    layer_out = (after_cross + out_near + out_far.astype(f32)).astype(bf16)
    feed_in_grad, feed_out_grad = call(
        finish_feed, (total["zero"], turn), [((d, units), f32), ((units, d), f32)], smem=(1,)
    )
    column, row = ((d, width), f32), ((width, d), f32)
    cross_grads = call(finish_heads, (total["one"], turn), [column, row, column, column], smem=(1,))
    self_grads = call(finish_heads, (total["two"], turn), [column, column, column, row], smem=(1,))
    gains = total["small"][:3]
    own_sums = lax.dynamic_slice(total["small"], (8 * (rank + 1), 0), (heads, TGT_LEN))
    bias_grad = lax.dot_general(hot, own_sums, (((0,), (1,)), ((), ())), precision=highest)

    return (
        layer_out,
        inputs_grad,
        memory_grad,
        gains[0],
        self_grads[0],
        self_grads[1],
        self_grads[2],
        self_grads[3],
        bias_grad,
        gains[1],
        cross_grads[0],
        cross_grads[2],
        cross_grads[3],
        cross_grads[1],
        gains[2],
        feed_in_grad,
        feed_out_grad,
    )


def solution(mesh):
    in_specs = (
        P(("dp", "mp"), None),
        P(("dp", "mp"), None),
        P("dp"),
        P("dp"),
        P(),
        P(),
        P(None, "mp"),
        P(None, "mp"),
        P(None, "mp"),
        P("mp", None),
        P(None, "mp"),
        P(),
        P(None, "mp"),
        P(None, "mp"),
        P(None, "mp"),
        P("mp", None),
        P(),
        P(None, "mp"),
        P("mp", None),
        P(("dp", "mp"), None),
    )
    out_specs = (
        P(("dp", "mp"), None),
        P(("dp", "mp"), None),
        P(("dp", "mp"), None),
        P(),
        P(None, "mp"),
        P(None, "mp"),
        P(None, "mp"),
        P("mp", None),
        P(None, "mp"),
        P(),
        P(None, "mp"),
        P(None, "mp"),
        P(None, "mp"),
        P("mp", None),
        P(),
        P(None, "mp"),
        P("mp", None),
    )
    return jax.shard_map(body, mesh=mesh, in_specs=in_specs, out_specs=out_specs, check_vma=False)
```

profile of v0, /device:TPU:0, one launch (start us, length us, event | category | flops | bytes accessed | tf_op | source)
XLA Modules:
  0.0 320.5 jit_solution(13972733144979935813)
XLA Ops:
  2.0 1.9 shard_map.323.n0
  3.9 2.9 collective-permute-start.1
  6.9 9.3 %collective-permute-done.1.n2 = bf16[256,768]{1,0:T(8,128)(2,1)S(1)} collective-permute-done((bf16[256,768]{1,0:T(8,128)(2,1)}, bf16[256,768]{1,0:T(8,128)(2,1)S(1)}, u32[]{:S(2)}, u32[]{:S(2)}) %collective-permute-start.1) | collective-permute-done | bytes 393248 | tf_op jit(solution)/shard_map/ppermute | solution.py:434
  17.1 1.9 copy.49.wq_ref
  24.4 9.1 %shard_map.324 = (bf16[1024,192]{1,0:T(8,128)(2,1)}, bf16[1024,192]{1,0:T(8,128)(2,1)}, bf16[1024,192]{1,0:T(8,128)(2,1)}, bf16[1024,192]{1,0:T(8,128)(2,1)}, f3...) custom-call(bf16[256,768]{1,0:T(8,128)(2,1)} %shard_map.323.n0, bf16[256,768]{1,0:T(8,128)(2,1)} %copy-done.36, ...), custom_call_target="tpu_custom_call" | custom-call | flops 1207959552 | bytes 6686244 | tf_op jit(solution)/shard_map/pallas_call | solution.py:409
  34.0 3.4 %collective-permute-done.5.w2 = bf16[384,768]{1,0:T(8,128)(2,1)S(1)} collective-permute-done((bf16[384,768]{1,0:T(8,128)(2,1)S(1)}, bf16[384,768]{1,0:T(8,128)(2,1)S(1)}, u32[]{:S(2)}, u32[]{:S(2)}) %collective-permute-start.5) | collective-permute-done | bytes 589856 | tf_op jit(solution)/shard_map/ppermute | solution.py:434
  37.5 1.8 collective-permute-start.6
  39.6 2.2 fusion.8
  43.4 5.8 %shard_map.325 = (bf16[1024,768]{1,0:T(8,128)(2,1)}, bf16[1024,768]{1,0:T(8,128)(2,1)}) custom-call(bf16[1024,768]{1,0:T(8,128)(2,1)} %mem_ref.2, bf16[384,768]{1,0:T(8,128)(2,1)} %copy-done.16, bf16[384,768]{1,0:T(8,128)(2,1)} %copy-done.32, bf16[384,768]{1,0:T(8,128)(2,1)} %copy-done.31, bf16[384,768]{1,0:T(8,128)(2,1)} %copy-done.33), custom_call_target="tpu_custom_call" | custom-call | flops 2415919104 | bytes 7077888 | tf_op jit(solution)/shard_map/pallas_call | solution.py:409
  49.3 4.1 %collective-permute-done.6.w2 = bf16[384,768]{1,0:T(8,128)(2,1)S(1)} collective-permute-done((bf16[384,768]{1,0:T(8,128)(2,1)S(1)}, bf16[384,768]{1,0:T(8,128)(2,1)S(1)}, u32[]{:S(2)}, u32[]{:S(2)}) %collective-permute-start.6) | collective-permute-done | bytes 589856 | tf_op jit(solution)/shard_map/ppermute | solution.py:434
  56.9 8.0 %collective-permute-done.4.far_ref = bf16[256,768]{1,0:T(8,128)(2,1)S(1)} collective-permute-done((bf16[256,768]{1,0:T(8,128)(2,1)S(1)}, bf16[256,768]{1,0:T(8,128)(2,1)S(1)}, u32[]{:S(2)}, u32[]{:S(2)}) %collective-permute-start.4) | collective-permute-done | bytes 393248 | tf_op jit(solution)/shard_map/ppermute | solution.py:434
  67.6 11.5 %shard_map.326 = (f32[256,768]{1,0:T(8,128)}, bf16[256,768]{1,0:T(8,128)(2,1)}, bf16[256,768]{1,0:T(8,128)(2,1)}, bf16[256,768]{1,0:T(8,128)(2,1)}, f32[256,768]{1,0:T(8,128)}, /*index=5*/bf16[256,768]{1,0:T(8,128)(2,1)}) custom-call(bf16[256,768]{1,0:T(8,128)(2,1)} %x_ref.5, f32[256,768]{1,0:T(8,128)} %get-tuple-element.249.near_ref, ...), custom_call_target="tpu_custom_call" | custom-call | flops 1811939328 | bytes 10229768 | tf_op jit(solution)/shard_map/pallas_call | solution.py:409
  80.0 9.8 %collective-permute-done.12.g2 = bf16[256,768]{1,0:T(8,128)(2,1)S(1)} collective-permute-done((bf16[256,768]{1,0:T(8,128)(2,1)}, bf16[256,768]{1,0:T(8,128)(2,1)S(1)}, u32[]{:S(2)}, u32[]{:S(2)}) %collective-permute-start.12) | collective-permute-done | bytes 393248 | tf_op jit(solution)/shard_map/ppermute | solution.py:434
  92.3 8.7 %shard_map.327 = (f32[256,768]{1,0:T(8,128)}, f32[256,768]{1,0:T(8,128)}, bf16[2,256,768]{2,1,0:T(8,128)(2,1)}, bf16[1024,768]{1,0:T(8,128)(2,1)}, bf16[1024,768]{1,0:T(8,128)(2,1)}) custom-call(bf16[256,768]{1,0:T(8,128)(2,1)} %get-tuple-element.122.g0, bf16[256,768]{1,0:T(8,128)(2,1)} %copy-done.41, bf16[256,768]{1,0:T(8,128)(2,1)} %copy-done.39, ...), custom_call_target="tpu_custom_call" | custom-call | flops 3623878656 | bytes 11010048 | tf_op jit(solution)/shard_map/pallas_call | solution.py:409
  101.1 2.4 collective-permute-done.17
  103.5 2.4 convert_add_fusion.4
  106.3 8.0 %shard_map.328 = (f32[256,768]{1,0:T(8,128)}, f32[256,768]{1,0:T(8,128)}, bf16[2,256,768]{2,1,0:T(8,128)(2,1)}, bf16[8,2,96,768]{3,2,1,0:T(8,128)(2,1)}) custom-call(bf16[256,768]{1,0:T(8,128)(2,1)} %get-tuple-element.122.g0, bf16[256,768]{1,0:T(8,128)(2,1)} %copy-done.41, bf16[256,768]{1,0:T(8,128)(2,1)} %copy-done.39, bf16[256,768]{1,0:T(8,128)(2,1)} %copy-done.44, ...), custom_call_target="tpu_custom_call" | custom-call | flops 3623878656 | bytes 12189700 | tf_op jit(solution)/shard_map/pallas_call | solution.py:409
  118.1 17.7 %shard_map.329 = (f32[256,768]{1,0:T(8,128)}, bf16[256,768]{1,0:T(8,128)(2,1)}, bf16[1024,768]{1,0:T(8,128)(2,1)}, bf16[1024,768]{1,0:T(8,128)(2,1)}, f32[2,768]...) custom-call(f32[256,768]{1,0:T(8,128)} %get-tuple-element.246.near_ref, ...), custom_call_target="tpu_custom_call" | custom-call | flops 4831838208 | bytes 16527372 | tf_op jit(solution)/shard_map/pallas_call | solution.py:409
  137.4 8.0 %shard_map.330 = (bf16[2,8,4,24,768]{4,3,2,1,0:T(8,128)(2,1)}, bf16[2,8,4,24,768]{4,3,2,1,0:T(8,128)(2,1)}) custom-call(bf16[1024,768]{1,0:T(8,128)(2,1)} %get-tuple-element.162.dk_ref, bf16[1024,768]{1,0:T(8,128)(2,1)} %get-tuple-element.142.dv_ref, bf16[1024,768]{1,0:T(8,128)(2,1)} %mem_ref.2, bf16[2,8,2,24,768]{4,3,2,1,0:T(8,128)(2,1)} %get-tuple-element.143.keep_in, ...), custom_call_target="tpu_custom_call" | custom-call | flops 2415919104 | bytes 11796484 | tf_op jit(solution)/shard_map/pallas_call | solution.py:409
  150.5 2.0 collective-permute-done.22
  154.2 13.3 %shard_map.331 = (bf16[8,4,24,768]{3,2,1,0:T(8,128)(2,1)}, f32[8,128]{1,0:T(8,128)}, f32[256,768]{1,0:T(8,128)}, f32[256,768]{1,0:T(8,128)}, bf16[2,256,768]{2,1,0:T(8,128)(2,1)}) custom-call(bf16[256,768]{1,0:T(8,128)(2,1)} %get-tuple-element.140.u0, bf16[256,768]{1,0:T(8,128)(2,1)} %copy-done.48, bf16[256,768]{1,0:T(8,128)(2,1)} %copy-done.45, ...), custom_call_target="tpu_custom_call" | custom-call | flops 3019898880 | bytes 9442856 | tf_op jit(solution)/shard_map/pallas_call | solution.py:409
  168.7 1.9 slice.152
  172.8 2.6 collective-permute-start.29
  177.5 6.8 %shard_map.332 = f32[1024,768]{1,0:T(8,128)} custom-call(bf16[1024,768]{1,0:T(8,128)(2,1)} %get-tuple-element.162.dk_ref, bf16[1024,768]{1,0:T(8,128)(2,1)} %get-tuple-element.142.dv_ref, bf16[384,768]{1,0:T(8,128)(2,1)} %copy-done.16, bf16[384,768]{1,0:T(8,128)(2,1)} %copy-done.32, bf16[384,768]{1,0:T(8,128)(2,1)} %copy-done.31, bf16[384,768]{1,0:T(8,128)(2,1)} %copy-done.33), custom_call_target="tpu_custom_call" | custom-call | flops 2415919104 | bytes 8650752 | tf_op jit(solution)/shard_map/pallas_call | solution.py:409
  184.3 4.5 %collective-permute-done.29 = bf16[1,2,96,768]{3,2,1,0:T(8,128)(2,1)} collective-permute-done((bf16[1,2,96,768]{3,2,1,0:T(8,128)(2,1)S(1)}, bf16[1,2,96,768]{3,2,1,0:T(8,128)(2,1)}, u32[]{:S(2)}, u32[]{:S(2)}) %collective-permute-start.29) | collective-permute-done | bytes 294944 | tf_op jit(solution)/shard_map/ppermute | solution.py:453
  190.0 9.7 %collective-permute-done.28 = bf16[8,4,24,768]{3,2,1,0:T(8,128)(2,1)} collective-permute-done((bf16[8,4,24,768]{3,2,1,0:T(8,128)(2,1)S(1)}, bf16[8,4,24,768]{3,2,1,0:T(8,128)(2,1)}, u32[]{:S(2)}, u32[]{:S(2)}) %collective-permute-start.28) | collective-permute-done | bytes 1179680 | tf_op jit(solution)/shard_map/ppermute | solution.py:434
  202.5 2.6 collective-permute-start.35
  205.2 2.3 collective-permute-done.26.far_ref
  207.6 2.9 shard_map.333
  210.5 6.8 %collective-permute-done.35 = bf16[1,2,96,768]{3,2,1,0:T(8,128)(2,1)S(1)} collective-permute-done((bf16[1,2,96,768]{3,2,1,0:T(8,128)(2,1)S(1)}, bf16[1,2,96,768]{3,2,1,0:T(8,128)(2,1)S(1)}, u32[]{:S(2)}, u32[]{:S(2)}) %collective-permute-start.35) | collective-permute-done | bytes 294944 | tf_op jit(solution)/shard_map/ppermute | solution.py:464
  219.6 18.3 %collective-permute-done.33 = bf16[2,4,24,768]{3,2,1,0:T(8,128)(2,1)S(1)} collective-permute-done((bf16[2,4,24,768]{3,2,1,0:T(8,128)(2,1)S(1)}, bf16[2,4,24,768]{3,2,1,0:T(8,128)(2,1)S(1)}, u32[]{:S(2)}, u32[]{:S(2)}) %collective-permute-start.33) | collective-permute-done | bytes 294944 | tf_op jit(solution)/shard_map/ppermute | solution.py:453
  242.5 3.4 %collective-permute-start.37 = (bf16[1,4,24,768]{3,2,1,0:T(8,128)(2,1)S(1)}, bf16[1,4,24,768]{3,2,1,0:T(8,128)(2,1)S(1)}, u32[]{:S(2)}, u32[]{:S(2)}) collective-permute-start(bf16[1,4,24,768]{3,2,1,0:T(8,128)(2,1)S(1)} %add_convert_fusion.15), channel_id=1, source_target_pairs={{0,16},{4,20},{8,24},{12,28},{16,0},{20,4},{24,8},{28,12},{1,17},{... | collective-permute-start | bytes 442376 | tf_op jit(solution)/shard_map/ppermute | solution.py:453
  245.9 2.7 collective-permute-done.38
  248.6 3.9 %collective-permute-start.42 = (bf16[1,4,24,768]{3,2,1,0:T(8,128)(2,1)S(1)}, bf16[1,4,24,768]{3,2,1,0:T(8,128)(2,1)S(1)}, u32[]{:S(2)}, u32[]{:S(2)}) collective-permute-start(bf16[1,4,24,768]{3,2,1,0:T(8,128)(2,1)S(1)} %add_convert_fusion.13), channel_id=1, source_target_pairs={{0,16},{4,20},{8,24},{12,28},{16,0},{20,4},{24,8},{28,12},{1,17},{... | collective-permute-start | bytes 442376 | tf_op jit(solution)/shard_map/ppermute | solution.py:453
  252.5 4.4 %collective-permute-done.37 = bf16[1,4,24,768]{3,2,1,0:T(8,128)(2,1)S(1)} collective-permute-done((bf16[1,4,24,768]{3,2,1,0:T(8,128)(2,1)S(1)}, bf16[1,4,24,768]{3,2,1,0:T(8,128)(2,1)S(1)}, u32[]{:S(2)}, u32[]{:S(2)}) %collective-permute-start.37) | collective-permute-done | bytes 147488 | tf_op jit(solution)/shard_map/ppermute | solution.py:453
  257.2 8.7 %collective-permute-done.43 = bf16[4,2,96,768]{3,2,1,0:T(8,128)(2,1)S(1)} collective-permute-done((bf16[4,2,96,768]{3,2,1,0:T(8,128)(2,1)S(1)}, bf16[4,2,96,768]{3,2,1,0:T(8,128)(2,1)S(1)}, u32[]{:S(2)}, u32[]{:S(2)}) %collective-permute-start.43) | collective-permute-done | bytes 1179680 | tf_op jit(solution)/shard_map/ppermute | solution.py:464
  267.5 4.5 %collective-permute-start.46 = (bf16[1,4,24,768]{3,2,1,0:T(8,128)(2,1)S(1)}, bf16[1,4,24,768]{3,2,1,0:T(8,128)(2,1)S(1)}, u32[]{:S(2)}, u32[]{:S(2)}) collective-permute-start(bf16[1,4,24,768]{3,2,1,0:T(8,128)(2,1)S(1)} %add_convert_fusion.10), channel_id=1, source_target_pairs={{0,16},{4,20},{8,24},{12,28},{16,0},{20,4},{24,8},{28,12},{1,17},{... | collective-permute-start | bytes 442376 | tf_op jit(solution)/shard_map/ppermute | solution.py:464
  278.3 4.3 %collective-permute-done.45 = bf16[2,4,24,768]{3,2,1,0:T(8,128)(2,1)S(1)} collective-permute-done((bf16[2,4,24,768]{3,2,1,0:T(8,128)(2,1)S(1)}, bf16[2,4,24,768]{3,2,1,0:T(8,128)(2,1)S(1)}, u32[]{:S(2)}, u32[]{:S(2)}) %collective-permute-start.45) | collective-permute-done | bytes 294944 | tf_op jit(solution)/shard_map/ppermute | solution.py:464
  284.6 2.5 collective-permute-start.44
  287.1 3.2 collective-permute-done.44
  293.1 1.9 fusion.5
  295.0 4.0 %shard_map.336 = (f32[768,768]{1,0:T(8,128)}, f32[768,768]{1,0:T(8,128)}) custom-call(bf16[8,2,96,768]{3,2,1,0:T(8,128)(2,1)} %pad_maximum_fusion.total_ref, s32[1]{0:T(128)} %bitcast.8.turn_ref), custom_call_target="tpu_custom_call" | custom-call | bytes 7077892 | tf_op jit(solution)/shard_map/pallas_call | solution.py:409
  299.0 2.2 pad_maximum_fusion.2.total_ref
  301.2 3.0 shard_map.334
  304.8 2.3 copy.55
  310.6 2.2 pad_maximum_fusion.3.total_ref
  312.8 3.2 shard_map.335
  316.0 2.3 copy.58
  (223 shorter events, 67.9 us)
Async XLA Ops:
  3.9 12.3 %collective-permute-start.1 = (bf16[256,768]{1,0:T(8,128)(2,1)}, bf16[256,768]{1,0:T(8,128)(2,1)S(1)}, u32[]{:S(2)}, u32[]{:S(2)}) collective-permute-start(bf16[256,768]{1,0:T(8,128)(2,1)} %shard_map.323.n0), channel_id=1, source_target_pairs={{0,2},{2,0},{1,3},{3,1},{4,6},{6,4},{5,7},{7,5},{8,10},{10,8},{9,1... | collective-permute-start | bytes 1179656 | tf_op jit(solution)/shard_map/ppermute | solution.py:434
  6.9 16.6 %collective-permute-start = (bf16[256,768]{1,0:T(8,128)(2,1)}, bf16[256,768]{1,0:T(8,128)(2,1)S(1)}, u32[]{:S(2)}, u32[]{:S(2)}) collective-permute-start(bf16[256,768]{1,0:T(8,128)(2,1)} %shard_map.323.n0), channel_id=1, source_target_pairs={{0,1},{1,0},{2,3},{3,2},{4,5},{5,4},{6,7},{7,6},{8,9},{9,8},{10,11... | collective-permute-start | bytes 1179656 | tf_op jit(solution)/shard_map/ppermute | solution.py:430
  16.2 7.3 %collective-permute-start.2 = (bf16[256,768]{1,0:T(8,128)(2,1)S(1)}, bf16[256,768]{1,0:T(8,128)(2,1)S(1)}, u32[]{:S(2)}, u32[]{:S(2)}) collective-permute-start(bf16[256,768]{1,0:T(8,128)(2,1)S(1)} %collective-permute-done.1.n2), channel_id=1, source_target_pairs={{0,1},{1,0},{2,3},{3,2},{4,5},{5,4},{6,7},{7,6},{8,9},{9,8},{10,11... | collective-permute-start | bytes 1179656 | tf_op jit(solution)/shard_map/ppermute | solution.py:430
  21.7 15.7 %collective-permute-start.5 = (bf16[384,768]{1,0:T(8,128)(2,1)S(1)}, bf16[384,768]{1,0:T(8,128)(2,1)S(1)}, u32[]{:S(2)}, u32[]{:S(2)}) collective-permute-start(bf16[384,768]{1,0:T(8,128)(2,1)S(1)} %pad_maximum_fusion.5.w0), channel_id=1, source_target_pairs={{0,2},{2,0},{1,3},{3,1},{4,6},{6,4},{5,7},{7,5},{8,10},{10,8},{9,1... | collective-permute-start | bytes 1769480 | tf_op jit(solution)/shard_map/ppermute | solution.py:434
  33.5 6.1 %collective-permute-start.3 = (bf16[2,256,768]{2,1,0:T(8,128)(2,1)}, bf16[2,256,768]{2,1,0:T(8,128)(2,1)S(1)}, u32[]{:S(2)}, u32[]{:S(2)}) collective-permute-start(bf16[2,256,768]{2,1,0:T(8,128)(2,1)} %get-tuple-element.110), channel_id=1, source_target_pairs={{0,1},{1,0},{2,3},{3,2},{4,5},{5,4},{6,7},{7,6},{8,9},{9,8},{10,11... | collective-permute-start | bytes 2359304 | tf_op jit(solution)/shard_map/ppermute | solution.py:430
  33.7 8.1 %collective-permute-start.7 = (bf16[384,768]{1,0:T(8,128)(2,1)S(1)}, bf16[384,768]{1,0:T(8,128)(2,1)S(1)}, u32[]{:S(2)}, u32[]{:S(2)}) collective-permute-start(bf16[384,768]{1,0:T(8,128)(2,1)S(1)} %pad_maximum_fusion.5.w0), channel_id=1, source_target_pairs={{0,1},{1,0},{2,3},{3,2},{4,5},{5,4},{6,7},{7,6},{8,9},{9,8},{10,11... | collective-permute-start | bytes 1769480 | tf_op jit(solution)/shard_map/ppermute | solution.py:430
  37.5 15.8 %collective-permute-start.6 = (bf16[384,768]{1,0:T(8,128)(2,1)S(1)}, bf16[384,768]{1,0:T(8,128)(2,1)S(1)}, u32[]{:S(2)}, u32[]{:S(2)}) collective-permute-start(bf16[384,768]{1,0:T(8,128)(2,1)S(1)} %pad_maximum_fusion.4.w0), channel_id=1, source_target_pairs={{0,2},{2,0},{1,3},{3,1},{4,6},{6,4},{5,7},{7,5},{8,10},{10,8},{9,1... | collective-permute-start | bytes 1769480 | tf_op jit(solution)/shard_map/ppermute | solution.py:434
  39.3 27.3 %collective-permute-start.9 = (bf16[384,768]{1,0:T(8,128)(2,1)S(1)}, bf16[384,768]{1,0:T(8,128)(2,1)S(1)}, u32[]{:S(2)}, u32[]{:S(2)}) collective-permute-start(bf16[384,768]{1,0:T(8,128)(2,1)S(1)} %pad_maximum_fusion.4.w0), channel_id=1, source_target_pairs={{0,1},{1,0},{2,3},{3,2},{4,5},{5,4},{6,7},{7,6},{8,9},{9,8},{10,11... | collective-permute-start | bytes 1769480 | tf_op jit(solution)/shard_map/ppermute | solution.py:430
  53.3 13.3 %collective-permute-start.10 = (bf16[384,768]{1,0:T(8,128)(2,1)S(1)}, bf16[384,768]{1,0:T(8,128)(2,1)S(1)}, u32[]{:S(2)}, u32[]{:S(2)}) collective-permute-start(bf16[384,768]{1,0:T(8,128)(2,1)S(1)} %collective-permute-done.6.w2), channel_id=1, source_target_pairs={{0,1},{1,0},{2,3},{3,2},{4,5},{5,4},{6,7},{7,6},{8,9},{9,8},{10,11... | collective-permute-start | bytes 1769480 | tf_op jit(solution)/shard_map/ppermute | solution.py:430
  53.3 11.5 %collective-permute-start.4 = (bf16[256,768]{1,0:T(8,128)(2,1)S(1)}, bf16[256,768]{1,0:T(8,128)(2,1)S(1)}, u32[]{:S(2)}, u32[]{:S(2)}) collective-permute-start(bf16[256,768]{1,0:T(8,128)(2,1)S(1)} %get-tuple-element.248), channel_id=1, source_target_pairs={{0,2},{2,0},{1,3},{3,1},{4,6},{6,4},{5,7},{7,5},{8,10},{10,8},{9,1... | collective-permute-start | bytes 1179656 | tf_op jit(solution)/shard_map/ppermute | solution.py:434
  64.9 15.0 %collective-permute-start.15 = (bf16[256,768]{1,0:T(8,128)(2,1)}, bf16[256,768]{1,0:T(8,128)(2,1)S(1)}, u32[]{:S(2)}, u32[]{:S(2)}) collective-permute-start(bf16[256,768]{1,0:T(8,128)(2,1)} %cot_ref.1), channel_id=1, source_target_pairs={{0,2},{2,0},{1,3},{3,1},{4,6},{6,4},{5,7},{7,5},{8,10},{10,8},{9,1... | collective-permute-start | bytes 1179656 | tf_op jit(solution)/shard_map/ppermute | solution.py:434
  79.1 10.7 %collective-permute-start.12 = (bf16[256,768]{1,0:T(8,128)(2,1)}, bf16[256,768]{1,0:T(8,128)(2,1)S(1)}, u32[]{:S(2)}, u32[]{:S(2)}) collective-permute-start(bf16[256,768]{1,0:T(8,128)(2,1)} %get-tuple-element.122.g0), channel_id=1, source_target_pairs={{0,2},{2,0},{1,3},{3,1},{4,6},{6,4},{5,7},{7,5},{8,10},{10,8},{9,1... | collective-permute-start | bytes 1179656 | tf_op jit(solution)/shard_map/ppermute | solution.py:434
  79.4 10.4 %collective-permute-start.14 = (bf16[256,768]{1,0:T(8,128)(2,1)S(1)}, bf16[256,768]{1,0:T(8,128)(2,1)S(1)}, u32[]{:S(2)}, u32[]{:S(2)}) collective-permute-start(bf16[256,768]{1,0:T(8,128)(2,1)S(1)} %copy-done.34), channel_id=1, source_target_pairs={{0,1},{1,0},{2,3},{3,2},{4,5},{5,4},{6,7},{7,6},{8,9},{9,8},{10,11... | collective-permute-start | bytes 1179656 | tf_op jit(solution)/shard_map/ppermute | solution.py:430
  79.4 10.4 %collective-permute-start.11 = (bf16[256,768]{1,0:T(8,128)(2,1)}, bf16[256,768]{1,0:T(8,128)(2,1)S(1)}, u32[]{:S(2)}, u32[]{:S(2)}) collective-permute-start(bf16[256,768]{1,0:T(8,128)(2,1)} %get-tuple-element.122.g0), channel_id=1, source_target_pairs={{0,1},{1,0},{2,3},{3,2},{4,5},{5,4},{6,7},{7,6},{8,9},{9,8},{10,11... | collective-permute-start | bytes 1179656 | tf_op jit(solution)/shard_map/ppermute | solution.py:430
  79.9 9.9 %collective-permute-start.16 = (bf16[256,768]{1,0:T(8,128)(2,1)S(1)}, bf16[256,768]{1,0:T(8,128)(2,1)S(1)}, u32[]{:S(2)}, u32[]{:S(2)}) collective-permute-start(bf16[256,768]{1,0:T(8,128)(2,1)S(1)} %collective-permute-done.15.c2), channel_id=1, source_target_pairs={{0,1},{1,0},{2,3},{3,2},{4,5},{5,4},{6,7},{7,6},{8,9},{9,8},{10,11... | collective-permute-start | bytes 1179656 | tf_op jit(solution)/shard_map/ppermute | solution.py:430
  105.9 11.5 %collective-permute-start.18 = (bf16[256,768]{1,0:T(8,128)(2,1)S(1)}, bf16[256,768]{1,0:T(8,128)(2,1)S(1)}, u32[]{:S(2)}, u32[]{:S(2)}) collective-permute-start(bf16[256,768]{1,0:T(8,128)(2,1)S(1)} %get-tuple-element.247), channel_id=1, source_target_pairs={{0,2},{2,0},{1,3},{3,1},{4,6},{6,4},{5,7},{7,5},{8,10},{10,8},{9,1... | collective-permute-start | bytes 1179656 | tf_op jit(solution)/shard_map/ppermute | solution.py:434
  115.6 31.8 %collective-permute-start.21 = (bf16[4,2,96,768]{3,2,1,0:T(8,128)(2,1)S(1)}, bf16[4,2,96,768]{3,2,1,0:T(8,128)(2,1)S(1)}, u32[]{:S(2)}, u32[]{:S(2)}) collective-permute-start(bf16[4,2,96,768]{3,2,1,0:T(8,128)(2,1)S(1)} %slice.143), channel_id=1, source_target_pairs={{0,4},{4,0},{8,12},{12,8},{16,20},{20,16},{24,28},{28,24},{1,5},{5... | collective-permute-start | bytes 3538952 | tf_op jit(solution)/shard_map/ppermute | solution.py:453
  135.8 10.9 %collective-permute-start.20 = (bf16[256,768]{1,0:T(8,128)(2,1)}, bf16[256,768]{1,0:T(8,128)(2,1)S(1)}, u32[]{:S(2)}, u32[]{:S(2)}) collective-permute-start(bf16[256,768]{1,0:T(8,128)(2,1)} %get-tuple-element.140.u0), channel_id=1, source_target_pairs={{0,2},{2,0},{1,3},{3,1},{4,6},{6,4},{5,7},{7,5},{8,10},{10,8},{9,1... | collective-permute-start | bytes 1179656 | tf_op jit(solution)/shard_map/ppermute | solution.py:434
  147.7 4.8 %collective-permute-start.22 = (bf16[2,8,4,24,768]{4,3,2,1,0:T(8,128)(2,1)}, bf16[2,8,4,24,768]{4,3,2,1,0:T(8,128)(2,1)S(1)}, u32[]{:S(2)}, u32[]{:S(2)}) collective-permute-start(bf16[2,8,4,24,768]{4,3,2,1,0:T(8,128)(2,1)} %get-tuple-element.149), channel_id=1, source_target_pairs={{0,1},{1,0},{2,3},{3,2},{4,5},{5,4},{6,7},{7,6},{8,9},{9,8},{10,11... | collective-permute-start | bytes 7077896 | tf_op jit(solution)/shard_map/ppermute | solution.py:430
  148.4 4.5 %collective-permute-start.19 = (bf16[256,768]{1,0:T(8,128)(2,1)S(1)}, bf16[256,768]{1,0:T(8,128)(2,1)S(1)}, u32[]{:S(2)}, u32[]{:S(2)}) collective-permute-start(bf16[256,768]{1,0:T(8,128)(2,1)S(1)} %copy-done.42), channel_id=1, source_target_pairs={{0,1},{1,0},{2,3},{3,2},{4,5},{5,4},{6,7},{7,6},{8,9},{9,8},{10,11... | collective-permute-start | bytes 1179656 | tf_op jit(solution)/shard_map/ppermute | solution.py:430
  148.6 4.9 %collective-permute-start.23 = (bf16[256,768]{1,0:T(8,128)(2,1)S(1)}, bf16[256,768]{1,0:T(8,128)(2,1)S(1)}, u32[]{:S(2)}, u32[]{:S(2)}) collective-permute-start(bf16[256,768]{1,0:T(8,128)(2,1)S(1)} %copy-done.46), channel_id=1, source_target_pairs={{0,1},{1,0},{2,3},{3,2},{4,5},{5,4},{6,7},{7,6},{8,9},{9,8},{10,11... | collective-permute-start | bytes 1179656 | tf_op jit(solution)/shard_map/ppermute | solution.py:430
  148.9 18.6 %collective-permute-start.24 = (bf16[2,2,96,768]{3,2,1,0:T(8,128)(2,1)S(1)}, bf16[2,2,96,768]{3,2,1,0:T(8,128)(2,1)}, u32[]{:S(2)}, u32[]{:S(2)}) collective-permute-start(bf16[2,2,96,768]{3,2,1,0:T(8,128)(2,1)S(1)} %get-tuple-element.239), channel_id=1, source_target_pairs={{0,8},{4,12},{8,0},{12,4},{16,24},{20,28},{24,16},{28,20},{1,9},{5... | collective-permute-start | bytes 1769480 | tf_op jit(solution)/shard_map/ppermute | solution.py:453
  170.6 4.7 %collective-permute-start.25 = (bf16[2,256,768]{2,1,0:T(8,128)(2,1)}, bf16[2,256,768]{2,1,0:T(8,128)(2,1)S(1)}, u32[]{:S(2)}, u32[]{:S(2)}) collective-permute-start(bf16[2,256,768]{2,1,0:T(8,128)(2,1)} %get-tuple-element.160), channel_id=1, source_target_pairs={{0,1},{1,0},{2,3},{3,2},{4,5},{5,4},{6,7},{7,6},{8,9},{9,8},{10,11... | collective-permute-start | bytes 2359304 | tf_op jit(solution)/shard_map/ppermute | solution.py:430
  170.8 28.9 %collective-permute-start.28 = (bf16[8,4,24,768]{3,2,1,0:T(8,128)(2,1)S(1)}, bf16[8,4,24,768]{3,2,1,0:T(8,128)(2,1)}, u32[]{:S(2)}, u32[]{:S(2)}) collective-permute-start(bf16[8,4,24,768]{3,2,1,0:T(8,128)(2,1)S(1)} %fusion.1), channel_id=1, source_target_pairs={{0,2},{2,0},{1,3},{3,1},{4,6},{6,4},{5,7},{7,5},{8,10},{10,8},{9,1... | collective-permute-start | bytes 3538952 | tf_op jit(solution)/shard_map/ppermute | solution.py:434
  172.3 32.8 %collective-permute-start.27 = (bf16[4,4,24,768]{3,2,1,0:T(8,128)(2,1)}, bf16[4,4,24,768]{3,2,1,0:T(8,128)(2,1)S(1)}, u32[]{:S(2)}, u32[]{:S(2)}) collective-permute-start(bf16[4,4,24,768]{3,2,1,0:T(8,128)(2,1)} %slice.152), channel_id=1, source_target_pairs={{0,4},{4,0},{8,12},{12,8},{16,20},{20,16},{24,28},{28,24},{1,5},{5... | collective-permute-start | bytes 1769480 | tf_op jit(solution)/shard_map/ppermute | solution.py:453
  172.8 16.0 %collective-permute-start.29 = (bf16[1,2,96,768]{3,2,1,0:T(8,128)(2,1)S(1)}, bf16[1,2,96,768]{3,2,1,0:T(8,128)(2,1)}, u32[]{:S(2)}, u32[]{:S(2)}) collective-permute-start(bf16[1,2,96,768]{3,2,1,0:T(8,128)(2,1)S(1)} %add_convert_fusion.9), channel_id=1, source_target_pairs={{0,16},{4,20},{8,24},{12,28},{16,0},{20,4},{24,8},{28,12},{1,17},{... | collective-permute-start | bytes 884744 | tf_op jit(solution)/shard_map/ppermute | solution.py:453
  176.6 31.0 %collective-permute-start.26 = (bf16[256,768]{1,0:T(8,128)(2,1)}, bf16[256,768]{1,0:T(8,128)(2,1)}, u32[]{:S(2)}, u32[]{:S(2)}) collective-permute-start(bf16[256,768]{1,0:T(8,128)(2,1)} %get-tuple-element.244), channel_id=1, source_target_pairs={{0,2},{2,0},{1,3},{3,1},{4,6},{6,4},{5,7},{7,5},{8,10},{10,8},{9,1... | collective-permute-start | bytes 1179656 | tf_op jit(solution)/shard_map/ppermute | solution.py:434
  201.5 18.0 %collective-permute-start.34 = (bf16[4,4,24,768]{3,2,1,0:T(8,128)(2,1)S(1)}, bf16[4,4,24,768]{3,2,1,0:T(8,128)(2,1)S(1)}, u32[]{:S(2)}, u32[]{:S(2)}) collective-permute-start(bf16[4,4,24,768]{3,2,1,0:T(8,128)(2,1)S(1)} %slice.191), channel_id=1, source_target_pairs={{0,4},{4,0},{8,12},{12,8},{16,20},{20,16},{24,28},{28,24},{1,5},{5... | collective-permute-start | bytes 1769480 | tf_op jit(solution)/shard_map/ppermute | solution.py:453
  202.5 14.8 %collective-permute-start.35 = (bf16[1,2,96,768]{3,2,1,0:T(8,128)(2,1)S(1)}, bf16[1,2,96,768]{3,2,1,0:T(8,128)(2,1)S(1)}, u32[]{:S(2)}, u32[]{:S(2)}) collective-permute-start(bf16[1,2,96,768]{3,2,1,0:T(8,128)(2,1)S(1)} %add_convert_fusion.7), channel_id=1, source_target_pairs={{0,16},{4,20},{8,24},{12,28},{16,0},{20,4},{24,8},{28,12},{1,17},{... | collective-permute-start | bytes 884744 | tf_op jit(solution)/shard_map/ppermute | solution.py:464
  217.4 20.7 %collective-permute-start.39 = (bf16[2,2,96,768]{3,2,1,0:T(8,128)(2,1)S(1)}, bf16[2,2,96,768]{3,2,1,0:T(8,128)(2,1)S(1)}, u32[]{:S(2)}, u32[]{:S(2)}) collective-permute-start(bf16[2,2,96,768]{3,2,1,0:T(8,128)(2,1)S(1)} %pad_maximum_fusion.6), channel_id=1, source_target_pairs={{0,8},{4,12},{8,0},{12,4},{16,24},{20,28},{24,16},{28,20},{1,9},{5... | collective-permute-start | bytes 1769480 | tf_op jit(solution)/shard_map/ppermute | solution.py:464
  218.1 19.8 %collective-permute-start.33 = (bf16[2,4,24,768]{3,2,1,0:T(8,128)(2,1)S(1)}, bf16[2,4,24,768]{3,2,1,0:T(8,128)(2,1)S(1)}, u32[]{:S(2)}, u32[]{:S(2)}) collective-permute-start(bf16[2,4,24,768]{3,2,1,0:T(8,128)(2,1)S(1)} %get-tuple-element.243), channel_id=1, source_target_pairs={{0,8},{4,12},{8,0},{12,4},{16,24},{20,28},{24,16},{28,20},{1,9},{5... | collective-permute-start | bytes 884744 | tf_op jit(solution)/shard_map/ppermute | solution.py:453
  219.5 18.5 %collective-permute-start.32 = (f32[40,768]{1,0:T(8,128)S(1)}, f32[40,768]{1,0:T(8,128)S(1)}, u32[]{:S(2)}, u32[]{:S(2)}) collective-permute-start(f32[40,768]{1,0:T(8,128)S(1)} %copy-done.27), channel_id=1, source_target_pairs={{0,1},{1,0},{2,3},{3,2},{4,5},{5,4},{6,7},{7,6},{8,9},{9,8},{10,11... | collective-permute-start | bytes 368648 | tf_op jit(solution)/shard_map/ppermute | solution.py:474
  238.2 27.7 %collective-permute-start.43 = (bf16[4,2,96,768]{3,2,1,0:T(8,128)(2,1)S(1)}, bf16[4,2,96,768]{3,2,1,0:T(8,128)(2,1)S(1)}, u32[]{:S(2)}, u32[]{:S(2)}) collective-permute-start(bf16[4,2,96,768]{3,2,1,0:T(8,128)(2,1)S(1)} %pad_maximum_fusion.1), channel_id=1, source_target_pairs={{0,4},{4,0},{8,12},{12,8},{16,20},{20,16},{24,28},{28,24},{1,5},{5... | collective-permute-start | bytes 3538952 | tf_op jit(solution)/shard_map/ppermute | solution.py:464
  239.3 9.3 %collective-permute-start.38 = (bf16[2,4,24,768]{3,2,1,0:T(8,128)(2,1)S(1)}, bf16[2,4,24,768]{3,2,1,0:T(8,128)(2,1)S(1)}, u32[]{:S(2)}, u32[]{:S(2)}) collective-permute-start(bf16[2,4,24,768]{3,2,1,0:T(8,128)(2,1)S(1)} %get-tuple-element.241), channel_id=1, source_target_pairs={{0,8},{4,12},{8,0},{12,4},{16,24},{20,28},{24,16},{28,20},{1,9},{5... | collective-permute-start | bytes 884744 | tf_op jit(solution)/shard_map/ppermute | solution.py:453
  241.1 32.5 %collective-permute-start.30 = (bf16[2,256,768]{2,1,0:T(8,128)(2,1)S(1)}, bf16[2,256,768]{2,1,0:T(8,128)(2,1)S(1)}, u32[]{:S(2)}, u32[]{:S(2)}) collective-permute-start(bf16[2,256,768]{2,1,0:T(8,128)(2,1)S(1)} %copy-done.30), channel_id=1, source_target_pairs={{0,1},{1,0},{2,3},{3,2},{4,5},{5,4},{6,7},{7,6},{8,9},{9,8},{10,11... | collective-permute-start | bytes 2359304 | tf_op jit(solution)/shard_map/ppermute | solution.py:430
  241.1 16.0 %collective-permute-start.36 = (f32[40,768]{1,0:T(8,128)S(1)}, f32[40,768]{1,0:T(8,128)S(1)}, u32[]{:S(2)}, u32[]{:S(2)}) collective-permute-start(f32[40,768]{1,0:T(8,128)S(1)} %add.162), channel_id=1, source_target_pairs={{0,2},{1,3},{2,0},{3,1},{4,6},{5,7},{6,4},{7,5},{8,10},{9,11},{10,... | collective-permute-start | bytes 368648 | tf_op jit(solution)/shard_map/ppermute | solution.py:474
  242.5 14.4 %collective-permute-start.37 = (bf16[1,4,24,768]{3,2,1,0:T(8,128)(2,1)S(1)}, bf16[1,4,24,768]{3,2,1,0:T(8,128)(2,1)S(1)}, u32[]{:S(2)}, u32[]{:S(2)}) collective-permute-start(bf16[1,4,24,768]{3,2,1,0:T(8,128)(2,1)S(1)} %add_convert_fusion.15), channel_id=1, source_target_pairs={{0,16},{4,20},{8,24},{12,28},{16,0},{20,4},{24,8},{28,12},{1,17},{... | collective-permute-start | bytes 442376 | tf_op jit(solution)/shard_map/ppermute | solution.py:453
  248.6 18.8 %collective-permute-start.42 = (bf16[1,4,24,768]{3,2,1,0:T(8,128)(2,1)S(1)}, bf16[1,4,24,768]{3,2,1,0:T(8,128)(2,1)S(1)}, u32[]{:S(2)}, u32[]{:S(2)}) collective-permute-start(bf16[1,4,24,768]{3,2,1,0:T(8,128)(2,1)S(1)} %add_convert_fusion.13), channel_id=1, source_target_pairs={{0,16},{4,20},{8,24},{12,28},{16,0},{20,4},{24,8},{28,12},{1,17},{... | collective-permute-start | bytes 442376 | tf_op jit(solution)/shard_map/ppermute | solution.py:453
  257.0 15.1 %collective-permute-start.41 = (bf16[1,4,24,768]{3,2,1,0:T(8,128)(2,1)S(1)}, bf16[1,4,24,768]{3,2,1,0:T(8,128)(2,1)S(1)}, u32[]{:S(2)}, u32[]{:S(2)}) collective-permute-start(bf16[1,4,24,768]{3,2,1,0:T(8,128)(2,1)S(1)} %add_convert_fusion.12), channel_id=1, source_target_pairs={{0,16},{4,20},{8,24},{12,28},{16,0},{20,4},{24,8},{28,12},{1,17},{... | collective-permute-start | bytes 442376 | tf_op jit(solution)/shard_map/ppermute | solution.py:464
  257.1 18.4 %collective-permute-start.40 = (f32[40,768]{1,0:T(8,128)S(1)}, f32[40,768]{1,0:T(8,128)S(1)}, u32[]{:S(2)}, u32[]{:S(2)}) collective-permute-start(f32[40,768]{1,0:T(8,128)S(1)} %add.167), channel_id=1, source_target_pairs={{0,4},{4,0},{8,12},{12,8},{16,20},{20,16},{24,28},{28,24},{1,5},{5... | collective-permute-start | bytes 368648 | tf_op jit(solution)/shard_map/ppermute | solution.py:474
  267.5 8.8 %collective-permute-start.46 = (bf16[1,4,24,768]{3,2,1,0:T(8,128)(2,1)S(1)}, bf16[1,4,24,768]{3,2,1,0:T(8,128)(2,1)S(1)}, u32[]{:S(2)}, u32[]{:S(2)}) collective-permute-start(bf16[1,4,24,768]{3,2,1,0:T(8,128)(2,1)S(1)} %add_convert_fusion.10), channel_id=1, source_target_pairs={{0,16},{4,20},{8,24},{12,28},{16,0},{20,4},{24,8},{28,12},{1,17},{... | collective-permute-start | bytes 442376 | tf_op jit(solution)/shard_map/ppermute | solution.py:464
  272.1 10.6 %collective-permute-start.45 = (bf16[2,4,24,768]{3,2,1,0:T(8,128)(2,1)S(1)}, bf16[2,4,24,768]{3,2,1,0:T(8,128)(2,1)S(1)}, u32[]{:S(2)}, u32[]{:S(2)}) collective-permute-start(bf16[2,4,24,768]{3,2,1,0:T(8,128)(2,1)S(1)} %pad_maximum_fusion.9), channel_id=1, source_target_pairs={{0,8},{4,12},{8,0},{12,4},{16,24},{20,28},{24,16},{28,20},{1,9},{5... | collective-permute-start | bytes 884744 | tf_op jit(solution)/shard_map/ppermute | solution.py:464
  274.4 18.7 %collective-permute-start.31 = (bf16[256,768]{1,0:T(8,128)(2,1)}, bf16[256,768]{1,0:T(8,128)(2,1)}, u32[]{:S(2)}, u32[]{:S(2)}) collective-permute-start(bf16[256,768]{1,0:T(8,128)(2,1)} %fusion.2), channel_id=1, source_target_pairs={{0,2},{2,0},{1,3},{3,1},{4,6},{6,4},{5,7},{7,5},{8,10},{10,8},{9,1... | collective-permute-start | bytes 1179656 | tf_op jit(solution)/shard_map/ppermute | solution.py:434
  277.1 14.2 %collective-permute-start.49 = (bf16[2,4,24,768]{3,2,1,0:T(8,128)(2,1)}, bf16[2,4,24,768]{3,2,1,0:T(8,128)(2,1)S(1)}, u32[]{:S(2)}, u32[]{:S(2)}) collective-permute-start(bf16[2,4,24,768]{3,2,1,0:T(8,128)(2,1)} %pad_maximum_fusion.10), channel_id=1, source_target_pairs={{0,8},{4,12},{8,0},{12,4},{16,24},{20,28},{24,16},{28,20},{1,9},{5... | collective-permute-start | bytes 884744 | tf_op jit(solution)/shard_map/ppermute | solution.py:464
  283.5 15.5 %collective-permute-start.48 = (bf16[4,4,24,768]{3,2,1,0:T(8,128)(2,1)}, bf16[4,4,24,768]{3,2,1,0:T(8,128)(2,1)}, u32[]{:S(2)}, u32[]{:S(2)}) collective-permute-start(bf16[4,4,24,768]{3,2,1,0:T(8,128)(2,1)} %pad_maximum_fusion.7), channel_id=1, source_target_pairs={{0,4},{4,0},{8,12},{12,8},{16,20},{20,16},{24,28},{28,24},{1,5},{5... | collective-permute-start | bytes 1769480 | tf_op jit(solution)/shard_map/ppermute | solution.py:464
  284.6 5.7 %collective-permute-start.44 = (f32[40,768]{1,0:T(8,128)}, f32[40,768]{1,0:T(8,128)}, u32[]{:S(2)}, u32[]{:S(2)}) collective-permute-start(f32[40,768]{1,0:T(8,128)} %add.170), channel_id=1, source_target_pairs={{0,8},{4,12},{8,0},{12,4},{16,24},{20,28},{24,16},{28,20},{1,9},{5... | collective-permute-start | bytes 368648 | tf_op jit(solution)/shard_map/ppermute | solution.py:474
  292.1 18.5 %collective-permute-start.50 = (bf16[4,4,24,768]{3,2,1,0:T(8,128)(2,1)}, bf16[4,4,24,768]{3,2,1,0:T(8,128)(2,1)}, u32[]{:S(2)}, u32[]{:S(2)}) collective-permute-start(bf16[4,4,24,768]{3,2,1,0:T(8,128)(2,1)} %pad_maximum_fusion.8), channel_id=1, source_target_pairs={{0,4},{4,0},{8,12},{12,8},{16,20},{20,16},{24,28},{28,24},{1,5},{5... | collective-permute-start | bytes 1769480 | tf_op jit(solution)/shard_map/ppermute | solution.py:464
  299.0 5.8 %collective-permute-start.47 = (f32[40,768]{1,0:T(8,128)S(1)}, f32[40,768]{1,0:T(8,128)S(1)}, u32[]{:S(2)}, u32[]{:S(2)}) collective-permute-start(f32[40,768]{1,0:T(8,128)S(1)} %add.171), channel_id=1, source_target_pairs={{0,16},{4,20},{8,24},{12,28},{16,0},{20,4},{24,8},{28,12},{1,17},{... | collective-permute-start | bytes 368648 | tf_op jit(solution)/shard_map/ppermute | solution.py:474
  (54 other events, 355.0 us)
where the time goes:
time: 321 us; the launch traced here: 320 us
  waiting for transfers between devices  108 us (34%)
  Pallas kernels  104 us (32%)
  starting transfers between devices  53.4 us (17%)
  local copies, waits for them, and re-layouts  27.1 us (8%)
  other arithmetic  24.8 us (8%)
    pallas_call x14, Pallas kernels, call(): pl.pallas_call(kernel, out_shape=[jax.ShapeDtypeStruct(s, t) for s, t in...  104 us
    ppermute x11, waiting for transfers between devices, swap_chip(): return lax.ppermute(a, 'mp', [(0, 2), (2, 0), (1, 3), (3, 1)])  48 us
    ppermute x9, waiting for transfers between devices, dp_chain(): got = lax.ppermute(send, 'dp', pairs)  29.9 us
    ppermute x9, waiting for transfers between devices, dp_chain(): other = lax.ppermute(value, 'dp', pairs)  20.1 us
    unnamed x111, local copies, waits for them, and re-layouts  20 us
    ppermute x9, starting transfers between devices, dp_chain(): got = lax.ppermute(send, 'dp', pairs)  17.8 us
    ppermute x11, starting transfers between devices, swap_chip(): return lax.ppermute(a, 'mp', [(0, 2), (2, 0), (1, 3), (3, 1)])  15.7 us
    ppermute x9, starting transfers between devices, dp_chain(): other = lax.ppermute(value, 'dp', pairs)  13.8 us
  transfers between devices with their start and end apart: 51, of which 23 were waited for; matrix products, arithmetic and copies ran while one was open for 10% of the time, Pallas kernels for 28%

commit v1 on v0

--- a/solution.py
+++ b/solution.py
@@ -54,6 +54,12 @@
         ref[(*lead, a ^ turn, index)] = grad[a * size : (a + 1) * size].astype(bf16)
 
 
+def store_halves(low_ref, high_ref, ref):
+    half = ref.shape[0] // 2
+    low_ref[...] = ref[:half]
+    high_ref[...] = ref[half:]
+
+
 def store_grad(keep_ref, send_ref, index, grad, turn):
     width = grad.shape[0] // 4
     for j in range(4):
@@ -120,12 +126,12 @@
         grads = stack_pair(m_ref[rows, cols], masks)
         key_block = k_ref[key_rows, cols]
         probs = probs_of(queries, key_block, example, pair)
-        dv_ref[key_rows, cols] = dot_tn(probs.astype(bf16), grads).astype(bf16)
+        dv_ref[cols, key_rows] = dot_tn(grads, probs.astype(bf16)).astype(bf16)
         prob_grad = dot_nt(grads, v_ref[key_rows, cols])
         score_grad = probs * (prob_grad - jnp.sum(probs * prob_grad, -1, keepdims=True))
         low = score_grad.astype(bf16)
         dq_ref[rows, cols] = unstack_pair(dot_nn(low, key_block)).astype(bf16)
-        dk_ref[key_rows, cols] = dot_tn(low, queries).astype(bf16)
+        dk_ref[cols, key_rows] = dot_tn(queries, low).astype(bf16)
         return carry
 
     lax.fori_loop(0, examples * pairs, step, 0, unroll=UNROLL_BACK)
@@ -172,7 +178,7 @@
 
 def first_norm(x_ref, gain_ref, n_ref):
     hidden = x_ref[...].astype(f32)
-    n_ref[...] = (hidden * row_scale(hidden) * gain_ref[...]).astype(bf16)
+    n_ref[...] = (hidden * row_scale(hidden) * gain_ref[...].reshape(1, -1)).astype(bf16)
 
 
 def store_parts(own_ref, chip_ref, send_ref, parts):
@@ -194,7 +200,7 @@
     for j, n in enumerate((n0, n1, n2, n3)):
         rows = slice(j * size, (j + 1) * size)
         for ref, w in ((q_ref, wq_ref), (k_ref, wk_ref), (v_ref, wv_ref)):
-            ref[rows, :] = dot_nn(n[...], w[...]).astype(bf16)
+            ref[rows, :] = dot_nt(n[...], w[...]).astype(bf16)
 
     def step(i, carry):
         rows = pl.ds(pl.multiple_of(i * TGT_LEN, TGT_LEN), TGT_LEN)
@@ -213,62 +219,61 @@
 def memory_forward(mem_ref, w0, w1, w2, w3, k_ref, v_ref):
     width = k_ref.shape[1] // 4
     blocks = (w0, w1, w2, w3)
-    k_ref[...] = dot_nt(mem_ref[...], matrix(blocks, 0, width)).astype(bf16)
-    v_ref[...] = dot_nt(mem_ref[...], matrix(blocks, 1, width)).astype(bf16)
+    k_ref[...] = dot_nt(mem_ref[...], matrix(blocks, 2, width)).astype(bf16)
+    v_ref[...] = dot_nt(mem_ref[...], matrix(blocks, 3, width)).astype(bf16)
 
 
 def cross_forward(
-    x_ref, near_ref, far_ref, k_ref, v_ref, gain_two_ref, gain_three_ref, w0, w1, w2, w3, len_ref,
+    x_ref, own_ref, near_ref, far_ref, k_ref, v_ref, gain_two_ref, gain_three_ref, w0, w1, w2, w3, rank_ref, len_ref,
     after_self_ref, n2_ref, q_ref, mixed_ref, after_ref, n3_ref,
 ):
     blocks = (w0, w1, w2, w3)
     width = q_ref.shape[1] // 4
-    after_self = x_ref[...].astype(f32) + near_ref[...] + far_ref[...].astype(f32)
+    after_self = x_ref[...].astype(f32) + own_ref[...] + near_ref[0].astype(f32) + far_ref[...].astype(f32)
     after_self_ref[...] = after_self
-    normed = (after_self * row_scale(after_self) * gain_two_ref[...]).astype(bf16)
+    normed = (after_self * row_scale(after_self) * gain_two_ref[...].reshape(1, -1)).astype(bf16)
     n2_ref[...] = normed
     q_ref[...] = dot_nt(normed, matrix(blocks, 0, width)).astype(bf16)
 
     def probs(queries, key_rows, example, pair):
-        return cross_probs(queries, key_rows, len_ref[example])
+        return cross_probs(queries, key_rows, len_ref[rank_ref[0] * (q_ref.shape[0] // TGT_LEN) + example])
 
     attend(q_ref, k_ref, v_ref, mixed_ref, MEM_LEN, probs)
     after = after_self_ref[...] + dot_nn(mixed_ref[...], matrix(blocks, 1, width))
     after_ref[...] = after
-    n3_ref[...] = (after * row_scale(after) * gain_three_ref[...]).astype(bf16)
-
-
-def feed_main(
-    g0, g1, g2, g3, c0, c1, c2, c3, in_ref, out_ref, own_ref, chip_ref, send_ref, act_ref, pre_grad_ref
-):
-    for j, (g, c) in enumerate(zip((g0, g1, g2, g3), (c0, c1, c2, c3))):
+    n3_ref[...] = (after * row_scale(after) * gain_three_ref[...].reshape(1, -1)).astype(bf16)
+
+
+def feed_hidden(c0, c1, c2, c3, out_ref, hidden_ref):
+    for j, c in enumerate((c0, c1, c2, c3)):
+        hidden_ref[j * c.shape[0] : (j + 1) * c.shape[0], :] = dot_nt(c[...], out_ref[...])
+
+
+def feed_main(g0, g1, g2, g3, hidden_ref, in_ref, own_ref, chip_ref, send_ref, act_ref, pre_grad_ref):
+    def part(j, g):
         rows = slice(j * g.shape[0], (j + 1) * g.shape[0])
         pre = dot_nn(g[...], in_ref[...])
-        hidden_grad = dot_nt(c[...], out_ref[...])
         square = pre * pre
         tanh = jnp.tanh(tanh_scale * (pre + cubic_term * square * pre))
         act_ref[rows, :] = (0.5 * pre * (1.0 + tanh)).astype(bf16)
         slope = 0.5 * (1.0 + tanh) + 0.5 * pre * (1.0 - tanh * tanh) * (
             tanh_scale * (1.0 + 3.0 * cubic_term * square)
         )
-        low = (hidden_grad * slope).astype(bf16)
+        low = (hidden_ref[rows, :] * slope).astype(bf16)
         pre_grad_ref[rows, :] = low
-        grad = dot_nt(low, in_ref[...])
-        if j == 0:
-            own_ref[...] = grad
-        elif j == 2:
-            chip_ref[...] = grad
-        else:
-            send_ref[j // 2] = grad.astype(bf16)
+        return dot_nt(low, in_ref[...])
+
+    store_parts(own_ref, chip_ref, send_ref, (part(j, g) for j, g in enumerate((g0, g1, g2, g3))))
 
 
 def feed_rest(
-    g0, g1, g2, g3, c0, c1, c2, c3, act_ref, pre_grad_ref, out_ref, turn_ref, own_ref, chip_ref, send_ref, grads_ref
+    g0, g1, g2, g3, c0, c1, c2, c3, act_ref, pre_grad_ref, out_ref, turn_ref, own_ref, chip_ref, send_ref, low_ref, high_ref, grads_ref
 ):
     gathered = jnp.concatenate([g[...] for g in (g0, g1, g2, g3)], 0)
     store_rows(grads_ref, (), 0, dot_tn(gathered, pre_grad_ref[...]), turn_ref[0])
     upstream = jnp.concatenate([c[...] for c in (c0, c1, c2, c3)], 0)
     store_rows(grads_ref, (), 1, dot_tn(act_ref[...], upstream), turn_ref[0])
+    store_halves(low_ref, high_ref, grads_ref)
     for j in range(4):
         rows = slice(j * g0.shape[0], (j + 1) * g0.shape[0])
         part = dot_nn(act_ref[rows, :], out_ref[...])
@@ -281,24 +286,24 @@
 
 
 def cross_backward(
-    near_ref, far_ref, cot_ref, after_ref, after_self_ref, gain_two_ref, gain_three_ref,
-    n2_ref, q_ref, k_ref, v_ref, mixed_ref, w0, w1, w2, w3, len_ref, turn_ref,
+    own_ref, near_ref, far_ref, cot_ref, after_ref, after_self_ref, gain_two_ref, gain_three_ref,
+    n2_ref, q_ref, k_ref, v_ref, mixed_ref, w0, w1, w2, w3, rank_ref, len_ref, turn_ref,
     grad_one_ref, up_ref, dk_ref, dv_ref, gains_ref, keep_ref, send_ref, m_ref, dq_ref,
 ):
     blocks = (w0, w1, w2, w3)
     width = q_ref.shape[1] // 4
     after = after_ref[...]
     scale = row_scale(after)
-    upstream = near_ref[...] + far_ref[...].astype(f32)
+    upstream = own_ref[...] + near_ref[0].astype(f32) + far_ref[...].astype(f32)
     gains_ref[1:2, :] = jnp.sum(upstream * after * scale, 0, keepdims=True)
-    grad_two = cot_ref[...].astype(f32) + norm_backward(after, scale, gain_three_ref[...], upstream)
+    grad_two = cot_ref[...].astype(f32) + norm_backward(after, scale, gain_three_ref[...].reshape(1, -1), upstream)
     grad_one_ref[...] = grad_two
     up_two = grad_two.astype(bf16)
     m_ref[...] = dot_nt(up_two, matrix(blocks, 1, width)).astype(bf16)
     store_grad(keep_ref, send_ref, 1, dot_tn(mixed_ref[...], up_two), turn_ref[0])
 
     def probs(queries, key_rows, example, pair):
-        return cross_probs(queries, key_rows, len_ref[example])
+        return cross_probs(queries, key_rows, len_ref[rank_ref[0] * (q_ref.shape[0] // TGT_LEN) + example])
 
     attend_back(q_ref, k_ref, v_ref, m_ref, dq_ref, dk_ref, dv_ref, MEM_LEN, probs)
     store_grad(keep_ref, send_ref, 0, dot_tn(dq_ref[...], n2_ref[...]), turn_ref[0])
@@ -306,7 +311,7 @@
     hidden = after_self_ref[...]
     scale = row_scale(hidden)
     gains_ref[0:1, :] = jnp.sum(upstream * hidden * scale, 0, keepdims=True)
-    grad_one = grad_one_ref[...] + norm_backward(hidden, scale, gain_two_ref[...], upstream)
+    grad_one = grad_one_ref[...] + norm_backward(hidden, scale, gain_two_ref[...].reshape(1, -1), upstream)
     grad_one_ref[...] = grad_one
     up_ref[...] = grad_one.astype(bf16)
 
@@ -317,14 +322,15 @@
         for a in range(keep_in.shape[1]):
             keep_ref[j, a, :count] = keep_in[j, a]
             send_ref[j, a, :count] = send_in[j, a]
-    store_grad(keep_ref, send_ref, count, dot_tn(dk_ref[...], mem_ref[...]), turn_ref[0])
-    store_grad(keep_ref, send_ref, count + 1, dot_tn(dv_ref[...], mem_ref[...]), turn_ref[0])
+    store_grad(keep_ref, send_ref, count, dot_nn(dk_ref[...], mem_ref[...]), turn_ref[0])
+    store_grad(keep_ref, send_ref, count + 1, dot_nn(dv_ref[...], mem_ref[...]), turn_ref[0])
 
 
 def self_backward(
     u0, u1, u2, u3, n0, n1, n2, n3, q_ref, k_ref, v_ref, mixed_ref, wq_ref, wk_ref, wv_ref, wo_ref,
     table_ref, rank_ref, len_ref, turn_ref,
-    grads_ref, sums_ref, own_ref, chip_ref, send_ref, bias_ref, score_ref, m_ref, dq_ref, dk_ref, dv_ref,
+    low_ref, high_ref, sums_ref, own_ref, chip_ref, send_ref,
+    bias_ref, score_ref, m_ref, dq_ref, dk_ref, dv_ref, grads_ref,
 ):
     fill_bias(table_ref, bias_ref)
     score_ref[...] = jnp.zeros_like(score_ref)
@@ -356,6 +362,7 @@
         ((dq_ref[...], normed), (dk_ref[...], normed), (dv_ref[...], normed), (mixed_ref[...], upstream))
     ):
         store_rows(grads_ref, (), index, dot_tn(left, right), turn_ref[0])
+    store_halves(low_ref, high_ref, grads_ref)
     heads = width // HEAD_DIM
     sums = [diagonal_sums(score_ref[h * TGT_LEN : (h + 1) * TGT_LEN, :]) for h in range(heads)]
     sums_ref[:heads, :] = jnp.concatenate(sums, 0)
@@ -363,14 +370,14 @@
 
     def part(j):
         rows = slice(j * size, (j + 1) * size)
-        out = dot_nt(dq_ref[rows, :], wq_ref[...])
-        return out + dot_nt(dk_ref[rows, :], wk_ref[...]) + dot_nt(dv_ref[rows, :], wv_ref[...])
+        out = dot_nn(dq_ref[rows, :], wq_ref[...])
+        return out + dot_nn(dk_ref[rows, :], wk_ref[...]) + dot_nn(dv_ref[rows, :], wv_ref[...])
 
     store_parts(own_ref, chip_ref, send_ref, (part(j) for j in range(4)))
 
 
-def last_norm(grad_one_ref, near_ref, far_ref, x_ref, gain_ref, late_ref, sums_ref, rank_ref, grad_ref, small_ref):
-    upstream = near_ref[...] + far_ref[...].astype(f32)
+def last_norm(grad_one_ref, own_ref, near_ref, far_ref, x_ref, gain_ref, late_ref, sums_ref, rank_ref, grad_ref, small_ref):
+    upstream = own_ref[...] + near_ref[0].astype(f32) + far_ref[...].astype(f32)
     hidden = x_ref[...].astype(f32)
     scale = row_scale(hidden)
     small_ref[...] = jnp.zeros_like(small_ref)
@@ -379,28 +386,28 @@
     for j in range(4):
         here = (rank_ref[0] == j).astype(f32)
         small_ref[8 * (j + 1) : 8 * (j + 2), :TGT_LEN] = sums_ref[...] * here
-    grad_ref[...] = grad_one_ref[...] + norm_backward(hidden, scale, gain_ref[...], upstream)
-
-
-def gather_rows(ref, index, turn):
-    return jnp.concatenate([ref[a ^ turn, index].astype(f32) for a in range(ref.shape[0])], 0)
-
-
-def finish_feed(total_ref, turn_ref, in_ref, out_ref):
-    in_ref[...] = gather_rows(total_ref, 0, turn_ref[0])
-    out_ref[...] = gather_rows(total_ref, 1, turn_ref[0])
-
-
-def finish_heads(total_ref, turn_ref, *outs):
+    grad_ref[...] = grad_one_ref[...] + norm_backward(hidden, scale, gain_ref[...].reshape(1, -1), upstream)
+
+
+def gather_rows(low_ref, high_ref, index, turn):
+    half = low_ref.shape[0]
+    pieces = []
+    for a in range(2 * half):
+        place = a ^ turn
+        inside = lax.rem(place, half)
+        pieces.append(jnp.where(place < half, low_ref[inside, index].astype(f32), high_ref[inside, index].astype(f32)))
+    return jnp.concatenate(pieces, 0)
+
+
+def finish(low_ref, high_ref, turn_ref, *outs):
     for index, ref in enumerate(outs):
-        rows = gather_rows(total_ref, index, turn_ref[0])
-        ref[...] = rows if ref.shape == rows.shape else rows.T
+        ref[...] = gather_rows(low_ref, high_ref, index, turn_ref[0])
 
 
 def memory_backward(dk_ref, dv_ref, w0, w1, w2, w3, grad_ref):
     blocks = (w0, w1, w2, w3)
-    width = dk_ref.shape[1] // 4
-    grad_ref[...] = dot_nn(dk_ref[...], matrix(blocks, 0, width)) + dot_nn(dv_ref[...], matrix(blocks, 1, width))
+    width = dk_ref.shape[0] // 4
+    grad_ref[...] = dot_tn(dk_ref[...], matrix(blocks, 2, width)) + dot_tn(dv_ref[...], matrix(blocks, 3, width))
 
 
 def call(kernel, operands, outs, scratch=(), flops=0, smem=()):
@@ -439,15 +446,14 @@
     return (a, swap_core(a), far, swap_core(far))
 
 
-def core_sum(own, chip, send):
+def core_sum(chip, send):
     got = swap_core(send)
-    return own.astype(f32) + got[0].astype(f32), (chip.astype(f32) + got[1].astype(f32)).astype(bf16)
-
-
-def dp_chain(value):
+    return got, (chip.astype(f32) + got[1].astype(f32)).astype(bf16)
+
+
+def dp_chain(keep, send):
     size = lax.axis_size("dp")
     bits = range(size.bit_length() - 1)
-    keep, send = value[: size // 2], value[size // 2 :]
     for bit in bits:
         pairs = [(i, i ^ (1 << bit)) for i in range(size)]
         got = lax.ppermute(send, "dp", pairs)
@@ -463,8 +469,10 @@
         pairs = [(i, i ^ (1 << bit)) for i in range(size)]
         other = lax.ppermute(value, "dp", pairs)
         token = yield value
-        value = jnp.concatenate([value, after(other, token)], 0)
-    yield value
+        other = after(other, token)
+        if bit:
+            value = jnp.concatenate([value, other], 0)
+    yield value, other
 
 
 def sum_all(value):
@@ -520,8 +528,6 @@
     turn = jnp.zeros((1,), jnp.int32)
     for bit in range(blocks.bit_length() - 1):
         turn = 2 * turn + ((place >> bit) & 1)
-    memory_len = lax.dynamic_slice_in_dim(memory_len, rank * examples, examples, 0)
-    gain_one, gain_two, gain_three = self_gain[None], cross_gain[None], feed_gain[None]
 
     distance = (TGT_LEN - jnp.arange(TGT_LEN, dtype=jnp.int32)) % TGT_LEN
     lookup = distance[:, None] == jnp.arange(TGT_LEN, dtype=jnp.int32)[None, :]
@@ -531,76 +537,81 @@
     big = (rows, d)
     head_rows = (rows, wide)
     key_heads = (key_rows, wide)
+    heads_key = (wide, key_rows)
     square = ((heads * TGT_LEN, TGT_LEN), f32)
     group_heads = (4 * rows, width)
     pack = ((2, rows, d), bf16)
     product = 2 * rows * d * wide
 
+    def grad_half(count, size):
+        return ((blocks // 2, count, size // blocks, d), bf16)
+
     def grad_rows(count, size, lead=()):
         return ((*lead, blocks, count, size // blocks, d), bf16)
 
-    second_own = jnp.concatenate([cross_key.T, cross_value.T], 0)
-    third_own = jnp.concatenate([cross_query.T, cross_out], 0)
-    normed_one = call(first_norm, (inputs, gain_one), [(big, bf16)])[0]
-    ones = gather_blocks(normed_one)
-    second_far = swap_chip(after(second_own, ones[2]))
-    self_q, self_k, self_v, self_mixed, near, chip, send = call(
+    cross_own = jnp.concatenate([cross_query.T, cross_out, cross_key.T, cross_value.T], 0)
+    normed_one = call(first_norm, (inputs, self_gain), [(big, bf16)])[0]
+    far = after(swap_chip(normed_one), by_distance)
+    ones = (normed_one, swap_core(normed_one), far, swap_core(far))
+    cross_far = swap_chip(after(cross_own, far))
+    self_q, self_k, self_v, self_mixed, own, chip, send = call(
         self_forward,
-        (*ones, self_query, self_key, self_value, self_out, by_distance, rank_value, target_len),
+        (*ones, self_query.T, self_key.T, self_value.T, self_out, by_distance, rank_value, target_len),
         [(group_heads, bf16)] * 4 + [(big, f32), (big, f32), pack],
         [square],
         flops=4 * product,
         smem=(9, 10),
     )
-    second_far = after(second_far, self_mixed)
-    third_far = swap_chip(after(third_own, second_far))
-    near, far_send = core_sum(near, chip, send)
+    near, far_send = core_sum(chip, send)
     far = swap_chip(far_send)
-    second = (second_own, swap_core(second_own), second_far, swap_core(second_far))
+    cross_far = after(cross_far, far_send)
+    cross = (cross_own, swap_core(cross_own), cross_far, swap_core(cross_far))
     cross_k, cross_v = call(
-        memory_forward, (after(memory, far_send), *second), [(key_heads, bf16)] * 2, flops=8 * product
-    )
-    third_far = after(third_far, cross_v)
-    third = (third_own, swap_core(third_own), third_far, swap_core(third_far))
-    far = after(far, third_far)
+        memory_forward, (memory, *cross), [(key_heads, bf16)] * 2, flops=8 * product
+    )
+    far = after(far, cross_v)
     ups_far = swap_chip(after(cotangent, far))
     after_self, normed_two, cross_q, cross_mixed, after_cross, normed_three = call(
         cross_forward,
-        (inputs, near, far, cross_k, cross_v, gain_two, gain_three, *third, memory_len),
+        (inputs, own, near, far, cross_k, cross_v, cross_gain, feed_gain, *cross, rank_value, memory_len),
         [(big, f32), (big, bf16), (head_rows, bf16), (head_rows, bf16), (big, f32), (big, bf16)],
         flops=6 * product,
-        smem=(11,),
+        smem=(12, 13),
     )
     ups_far = after(ups_far, normed_three)
     ups = (cotangent, swap_core(cotangent), ups_far, swap_core(ups_far))
-    gathered = gather_blocks(normed_three)
     many = 4 * rows
-    near, chip, send, activated, pre_grad = call(
+    far = swap_chip(normed_three)
+    hidden = call(feed_hidden, (*ups, feed_output), [((many, units), f32)], flops=4 * product)[0]
+    far = after(far, hidden)
+    gathered = (normed_three, swap_core(normed_three), far, swap_core(far))
+    own, chip, send, activated, pre_grad = call(
         feed_main,
-        (*gathered, *ups, feed_input, feed_output),
+        (*gathered, hidden, feed_input),
         [(big, f32), (big, f32), pack, ((many, units), bf16), ((many, units), bf16)],
         flops=12 * product,
     )
-    near, far_send = core_sum(near, chip, send)
+    near, far_send = core_sum(chip, send)
     far = swap_chip(far_send)
-    out_near, out_chip, out_send, feed_part = call(
+    out_own, out_chip, out_send, low, high = call(
         feed_rest,
         (*gathered, *ups, after(activated, far_send), pre_grad, feed_output, turn),
-        [(big, f32), (big, f32), pack, grad_rows(2, d)],
+        [(big, f32), (big, f32), pack] + [grad_half(2, d)] * 2,
+        [grad_rows(2, d)],
         flops=12 * product,
         smem=(11,),
     )
-    zero = dp_chain(feed_part)
+    zero = dp_chain(low, high)
     token = next(zero)
     far = after(far, token)
     grad_one, up_one, key_grad, value_grad, late_gains, keep, send = call(
         cross_backward,
-        (near, far, cotangent, after_cross, after_self, gain_two, gain_three)
-        + (normed_two, cross_q, cross_k, cross_v, cross_mixed, *third, memory_len, turn),
-        [(big, f32), (big, bf16), (key_heads, bf16), (key_heads, bf16), ((2, d), f32)] + [grad_rows(2, width, (2,))] * 2,
+        (own, near, far, cotangent, after_cross, after_self, cross_gain, feed_gain)
+        + (normed_two, cross_q, cross_k, cross_v, cross_mixed, *cross, rank_value, memory_len, turn),
+        [(big, f32), (big, bf16), (heads_key, bf16), (heads_key, bf16), ((2, d), f32)] + [grad_rows(2, width, (2,))] * 2,
         [(head_rows, bf16), (head_rows, bf16)],
         flops=16 * product,
-        smem=(16, 17),
+        smem=(17, 18, 19),
     )
     up_far = swap_chip(up_one)
     keep, send = call(
@@ -612,61 +623,60 @@
     )
     up_far = after(up_far, keep)
     token = zero.send(up_far)
-    one_near, one_send = core_sum(keep[0], keep[1], after(send, token))
+    one_near, one_send = core_sum(keep[1], after(send, token))
     one_far = swap_chip(one_send)
     self_ups = (up_one, swap_core(up_one), after(up_far, one_send), swap_core(up_far))
-    grads, sums, near, chip, send = call(
+    low, high, sums, own, chip, send = call(
         self_backward,
         (*self_ups, *ones, self_q, self_k, self_v, self_mixed)
-        + (self_query, self_key, self_value, self_out, by_distance, rank_value, target_len, turn),
-        [grad_rows(4, width), ((8, TGT_LEN), f32), (big, f32), (big, f32), pack],
-        [square, square] + [(group_heads, bf16)] * 4,
+        + (self_query.T, self_key.T, self_value.T, self_out, by_distance, rank_value, target_len, turn),
+        [grad_half(4, width)] * 2 + [((8, TGT_LEN), f32), (big, f32), (big, f32), pack],
+        [square, square] + [(group_heads, bf16)] * 4 + [grad_rows(4, width)],
         flops=10 * product,
         smem=(17, 18, 19),
     )
-    token = zero.send(sums)
-    two = dp_chain(after(grads, token))
-    two_token = next(two)
-    near, far_send = core_sum(near, chip, after(send, two_token))
-    far = swap_chip(far_send)
     memory_grad = call(
         memory_backward,
-        (after(key_grad, far_send), value_grad, *second),
+        (after(key_grad, sums), value_grad, *cross),
         [((key_rows, d), f32)],
         flops=8 * product,
     )[0]
     token = zero.send(memory_grad)
-    one = dp_chain((one_near + after(one_far, token).astype(f32)).astype(bf16))
+    two = dp_chain(low, after(high, token))
+    token = next(two)
+    near, far_send = core_sum(chip, after(send, token))
+    far = swap_chip(far_send)
+    one_sum = (keep[0].astype(f32) + one_near[0].astype(f32) + after(one_far, far_send).astype(f32)).astype(bf16)
+    one = dp_chain(one_sum[: blocks // 2], one_sum[blocks // 2 :])
     token = next(one)
+    token = zero.send(token)
     token = two.send(token)
     inputs_grad, small = call(
         last_norm,
-        (grad_one, near, after(far, token), inputs, gain_one, late_gains, sums, rank_value),
+        (grad_one, own, near, after(far, token), inputs, self_gain, late_gains, sums, rank_value),
         [(big, f32), ((40, d), f32)],
-        smem=(7,),
+        smem=(8,),
     )
     small = sum_all(small)
     token = next_step(small, inputs_grad, True)
-    out_near, out_send = core_sum(out_near, out_chip, after(out_send, token))
+    out_near, out_send = core_sum(out_chip, after(out_send, token))
     out_far = swap_chip(out_send)
     total = {}
-    waiting = [(zero, "zero"), (one, "one"), (two, "two"), (small, "small")]
+    waiting = [(zero, "zero"), (two, "two"), (one, "one"), (small, "small")]
     while waiting:
         still = []
         for chain, name in waiting:
             step = next_step(chain, token)
             if step is None:
                 continue
-            token = total[name] = step
+            total[name] = step
+            token = step[1] if name != "small" and isinstance(step, tuple) else step
             still.append((chain, name))
         waiting = still
-    layer_out = (after_cross + out_near + out_far.astype(f32)).astype(bf16)
-    feed_in_grad, feed_out_grad = call(
-        finish_feed, (total["zero"], turn), [((d, units), f32), ((units, d), f32)], smem=(1,)
-    )
-    column, row = ((d, width), f32), ((width, d), f32)
-    cross_grads = call(finish_heads, (total["one"], turn), [column, row, column, column], smem=(1,))
-    self_grads = call(finish_heads, (total["two"], turn), [column, column, column, row], smem=(1,))
+    layer_out = (after_cross + out_own + out_near[0].astype(f32) + out_far.astype(f32)).astype(bf16)
+    feed_grads = call(finish, (*total["zero"], turn), [((d, units), f32), ((units, d), f32)], smem=(2,))
+    cross_grads = call(finish, (*total["one"], turn), [((width, d), f32)] * 4, smem=(2,))
+    self_grads = call(finish, (*total["two"], turn), [((width, d), f32)] * 4, smem=(2,))
     gains = total["small"][:3]
     own_sums = lax.dynamic_slice(total["small"], (8 * (rank + 1), 0), (heads, TGT_LEN))
     bias_grad = lax.dot_general(hot, own_sums, (((0,), (1,)), ((), ())), precision=highest)
@@ -676,19 +686,18 @@
         inputs_grad,
         memory_grad,
         gains[0],
-        self_grads[0],
-        self_grads[1],
-        self_grads[2],
+        self_grads[0].T,
+        self_grads[1].T,
+        self_grads[2].T,
         self_grads[3],
         bias_grad,
         gains[1],
-        cross_grads[0],
-        cross_grads[2],
-        cross_grads[3],
+        cross_grads[0].T,
+        cross_grads[2].T,
+        cross_grads[3].T,
         cross_grads[1],
         gains[2],
-        feed_in_grad,
-        feed_out_grad,
+        *feed_grads,
     )
 
 

time: 321 us -> 282 us (0.88)
  local copies, waits for them, and re-layouts: 27.1 us -> 7.97 us
  other arithmetic: 24.8 us -> 13.7 us
  waiting for transfers between devices: 108 us -> 99.1 us
  Pallas kernels: 104 us -> 112 us
  starting transfers between devices: 53.4 us -> 46.5 us
    ppermute x11 -> x10, waiting for transfers between devices: 48 us -> 28.3 us  [swap_chip(): return lax.ppermute(a, 'mp', [(0, 2), (2, 0), (1, 3), (3, 1)])]
    ppermute x9, waiting for transfers between devices: 20.1 us -> 36.5 us  [dp_chain(): other = lax.ppermute(value, 'dp', pairs)]
    unnamed x111 -> x82, local copies, waits for them, and re-layouts: 20 us -> 7.31 us
    ppermute x9, waiting for transfers between devices: 29.9 us -> 17.6 us  [dp_chain(): got = lax.ppermute(send, 'dp', pairs)]
    pallas_call x14 -> x15, Pallas kernels: 104 us -> 112 us  [call(): pl.pallas_call(kernel, out_shape=[jax.ShapeDtypeStruct(s, t) for s, t in...]
    concatenate x11 -> x7, other arithmetic: 8.77 us -> 2.97 us  [the longest x6 1.52 us: dp_chain(): value = jnp.concatenate([value, other], 0)]
    ppermute x9, starting transfers between devices: 17.8 us -> 13.2 us  [dp_chain(): got = lax.ppermute(send, 'dp', pairs)]
    ppermute x17 -> x15, waiting for transfers between devices: 6.71 us -> 10.5 us  [swap_core(): return lax.ppermute(a, 'mp', [(0, 1), (1, 0), (2, 3), (3, 2)])]
  transfers between devices with their start and end apart: 51 -> 48, of which waited for: 23 -> 24; matrix products, arithmetic and copies ran while one was open for 10% -> 5% of each run, Pallas kernels for 28% -> 35%
where the time goes in v1:
time: 282 us
  Pallas kernels  112 us (40%)
  waiting for transfers between devices  99.1 us (35%)
  starting transfers between devices  46.5 us (16%)
  other arithmetic  13.7 us (5%)
  local copies, waits for them, and re-layouts  7.97 us (3%)
    pallas_call x15, Pallas kernels, call(): pl.pallas_call(kernel, out_shape=[jax.ShapeDtypeStruct(s, t) for s, t in...  112 us
    ppermute x9, waiting for transfers between devices, dp_chain(): other = lax.ppermute(value, 'dp', pairs)  36.5 us
    ppermute x10, waiting for transfers between devices, swap_chip(): return lax.ppermute(a, 'mp', [(0, 2), (2, 0), (1, 3), (3, 1)])  28.3 us
    ppermute x9, waiting for transfers between devices, dp_chain(): got = lax.ppermute(send, 'dp', pairs)  17.6 us
    ppermute x10, starting transfers between devices, swap_chip(): return lax.ppermute(a, 'mp', [(0, 2), (2, 0), (1, 3), (3, 1)])  13.6 us
    ppermute x9, starting transfers between devices, dp_chain(): got = lax.ppermute(send, 'dp', pairs)  13.2 us
    ppermute x9, starting transfers between devices, dp_chain(): other = lax.ppermute(value, 'dp', pairs)  12.2 us
    ppermute x15, waiting for transfers between devices, swap_core(): return lax.ppermute(a, 'mp', [(0, 1), (1, 0), (2, 3), (3, 2)])  10.5 us
  transfers between devices with their start and end apart: 48, of which 24 were waited for; matrix products, arithmetic and copies ran while one was open for 5% of the time, Pallas kernels for 35%

profile of v1, /device:TPU:0, one launch (start us, length us, event | category | flops | bytes accessed | tf_op | source)
XLA Modules:
  0.0 281.7 jit_solution(15845335134530209142)
XLA Ops:
  0.7 1.9 shard_map.323.n0
  2.6 2.9 %collective-permute-start.1 = (bf16[256,768]{1,0:T(8,128)(2,1)}, bf16[256,768]{1,0:T(8,128)(2,1)S(1)}, u32[]{:S(2)}, u32[]{:S(2)}) collective-permute-start(bf16[256,768]{1,0:T(8,128)(2,1)} %shard_map.323.n0), channel_id=1, source_target_pairs={{0,2},{2,0},{1,3},{3,1},{4,6},{6,4},{5,7},{7,5},{8,10},{10,8},{9,1... | collective-permute-start | bytes 1179656 | tf_op jit(solution)/shard_map/ppermute | solution.py:441
  7.2 7.6 %collective-permute-done.1.n2 = bf16[256,768]{1,0:T(8,128)(2,1)S(1)} collective-permute-done((bf16[256,768]{1,0:T(8,128)(2,1)}, bf16[256,768]{1,0:T(8,128)(2,1)S(1)}, u32[]{:S(2)}, u32[]{:S(2)}) %collective-permute-start.1) | collective-permute-done | bytes 393248 | tf_op jit(solution)/shard_map/ppermute | solution.py:441
  16.3 1.8 collective-permute-start.6
  18.9 9.0 %shard_map.324 = (bf16[1024,192]{1,0:T(8,128)(2,1)}, bf16[1024,192]{1,0:T(8,128)(2,1)}, bf16[1024,192]{1,0:T(8,128)(2,1)}, bf16[1024,192]{1,0:T(8,128)(2,1)}, f3...) custom-call(bf16[256,768]{1,0:T(8,128)(2,1)} %shard_map.323.n0, bf16[256,768]{1,0:T(8,128)(2,1)} %copy-done.33, ...), custom_call_target="tpu_custom_call" | custom-call | flops 1207959552 | bytes 6686244 | tf_op jit(solution)/shard_map/pallas_call | solution.py:416
  28.4 2.3 collective-permute-done.3.near_ref
  30.7 1.5 fusion.7
  32.2 12.4 %collective-permute-done.6.w2 = bf16[768,768]{1,0:T(8,128)(2,1)S(1)} collective-permute-done((bf16[768,768]{1,0:T(8,128)(2,1)S(1)}, bf16[768,768]{1,0:T(8,128)(2,1)S(1)}, u32[]{:S(2)}, u32[]{:S(2)}) %collective-permute-start.6) | collective-permute-done | bytes 1179680 | tf_op jit(solution)/shard_map/ppermute | solution.py:441
  44.6 1.7 collective-permute-start.4
  48.6 6.6 %shard_map.325 = (bf16[1024,768]{1,0:T(8,128)(2,1)}, bf16[1024,768]{1,0:T(8,128)(2,1)}) custom-call(bf16[1024,768]{1,0:T(8,128)(2,1)} %mem_ref.3, bf16[768,768]{1,0:T(8,128)(2,1)} %copy-done.2, bf16[768,768]{1,0:T(8,128)(2,1)} %copy-done.4, bf16[768,768]{1,0:T(8,128)(2,1)} %copy-done.3, bf16[768,768]{1,0:T(8,128)(2,1)} %copy-done.5), custom_call_target="tpu_custom_call" | custom-call | flops 2415919104 | bytes 9437184 | tf_op jit(solution)/shard_map/pallas_call | solution.py:416
  56.2 1.7 collective-permute-start.11
  57.9 12.4 %shard_map.326 = (f32[256,768]{1,0:T(8,128)}, bf16[256,768]{1,0:T(8,128)(2,1)}, bf16[256,768]{1,0:T(8,128)(2,1)}, bf16[256,768]{1,0:T(8,128)(2,1)}, f32[256,768]{1,0:T(8,128)}, /*index=5*/bf16[256,768]{1,0:T(8,128)(2,1)}) custom-call(bf16[256,768]{1,0:T(8,128)(2,1)} %x_ref.5, f32[256,768]{1,0:T(8,128)} %get-tuple-element.111.own_ref, ...), custom_call_target="tpu_custom_call" | custom-call | flops 1811939328 | bytes 13375524 | tf_op jit(solution)/shard_map/pallas_call | solution.py:416
  73.1 4.8 %shard_map.327.hidden_ref = f32[1024,768]{1,0:T(8,128)} custom-call(bf16[256,768]{1,0:T(8,128)(2,1)} %cot_ref.1, bf16[256,768]{1,0:T(8,128)(2,1)} %copy-done.26, bf16[256,768]{1,0:T(8,128)(2,1)} %copy-done.25, bf16[256,768]{1,0:T(8,128)(2,1)} %copy-done.27, bf16[768,768]{1,0:T(8,128)(2,1)} %out_ref.3), custom_call_target="tpu_custom_call" | custom-call | flops 1207959552 | bytes 5898240 | tf_op jit(solution)/shard_map/pallas_call | solution.py:416
  77.9 4.4 %collective-permute-done.9.g2 = bf16[256,768]{1,0:T(8,128)(2,1)S(1)} collective-permute-done((bf16[256,768]{1,0:T(8,128)(2,1)}, bf16[256,768]{1,0:T(8,128)(2,1)S(1)}, u32[]{:S(2)}, u32[]{:S(2)}) %collective-permute-start.9) | collective-permute-done | bytes 393248 | tf_op jit(solution)/shard_map/ppermute | solution.py:441
  82.3 1.7 collective-permute-done.13.g3
  84.8 8.0 %shard_map.328 = (f32[256,768]{1,0:T(8,128)}, f32[256,768]{1,0:T(8,128)}, bf16[2,256,768]{2,1,0:T(8,128)(2,1)}, bf16[1024,768]{1,0:T(8,128)(2,1)}, bf16[1024,768]{1,0:T(8,128)(2,1)}) custom-call(bf16[256,768]{1,0:T(8,128)(2,1)} %get-tuple-element.120.g0, bf16[256,768]{1,0:T(8,128)(2,1)} %copy-done.36, bf16[256,768]{1,0:T(8,128)(2,1)} %copy-done.34, ...), custom_call_target="tpu_custom_call" | custom-call | flops 3623878656 | bytes 11403264 | tf_op jit(solution)/shard_map/pallas_call | solution.py:416
  92.9 2.4 collective-permute-done.14.near_ref
  97.5 8.1 %shard_map.329 = (f32[256,768]{1,0:T(8,128)}, f32[256,768]{1,0:T(8,128)}, bf16[2,256,768]{2,1,0:T(8,128)(2,1)}, bf16[4,2,96,768]{3,2,1,0:T(8,128)(2,1)}, bf16[4,2,96,768]{3,2,1,0:T(8,128)(2,1)}) custom-call(bf16[256,768]{1,0:T(8,128)(2,1)} %get-tuple-element.120.g0, bf16[256,768]{1,0:T(8,128)(2,1)} %copy-done.36, bf16[256,768]{1,0:T(8,128)(2,1)} %copy-done.34, ...), custom_call_target="tpu_custom_call" | custom-call | flops 3623878656 | bytes 12189700 | tf_op jit(solution)/shard_map/pallas_call | solution.py:416
  105.6 1.6 collective-permute-start.18
  108.8 19.3 %shard_map.330 = (f32[256,768]{1,0:T(8,128)}, bf16[256,768]{1,0:T(8,128)(2,1)}, bf16[768,1024]{1,0:T(8,128)(2,1)}, bf16[768,1024]{1,0:T(8,128)(2,1)}, f32[2,768]...) custom-call(f32[256,768]{1,0:T(8,128)} %get-tuple-element.131.own_ref, ...), custom_call_target="tpu_custom_call" | custom-call | flops 4831838208 | bytes 19673128 | tf_op jit(solution)/shard_map/pallas_call | solution.py:416
  128.8 7.9 %shard_map.331 = (bf16[2,8,4,24,768]{4,3,2,1,0:T(8,128)(2,1)}, bf16[2,8,4,24,768]{4,3,2,1,0:T(8,128)(2,1)}) custom-call(bf16[768,1024]{1,0:T(8,128)(2,1)} %get-tuple-element.159.dk_ref, bf16[768,1024]{1,0:T(8,128)(2,1)} %get-tuple-element.141.dv_ref, bf16[1024,768]{1,0:T(8,128)(2,1)} %mem_ref.3, bf16[2,8,2,24,768]{4,3,2,1,0:T(8,128)(2,1)} %get-tuple-element.142.keep_in, ...), custom_call_target="tpu_custom_call" | custom-call | flops 2415919104 | bytes 11796484 | tf_op jit(solution)/shard_map/pallas_call | solution.py:416
  136.7 2.1 collective-permute-done.17.u2
  140.3 1.6 collective-permute-start.21
  141.9 2.0 collective-permute-done.19
  146.6 13.2 %shard_map.332 = (bf16[4,4,24,768]{3,2,1,0:T(8,128)(2,1)}, bf16[4,4,24,768]{3,2,1,0:T(8,128)(2,1)}, f32[8,128]{1,0:T(8,128)}, f32[256,768]{1,0:T(8,128)}, f32[25...) custom-call(bf16[256,768]{1,0:T(8,128)(2,1)} %get-tuple-element.139.u0, bf16[256,768]{1,0:T(8,128)(2,1)} %copy-done.38, ...), custom_call_target="tpu_custom_call" | custom-call | flops 3019898880 | bytes 9442856 | tf_op jit(solution)/shard_map/pallas_call | solution.py:416
  159.8 7.6 %shard_map.333 = f32[1024,768]{1,0:T(8,128)} custom-call(bf16[768,1024]{1,0:T(8,128)(2,1)} %get-tuple-element.159.dk_ref, bf16[768,1024]{1,0:T(8,128)(2,1)} %get-tuple-element.141.dv_ref, bf16[768,768]{1,0:T(8,128)(2,1)} %copy-done.2, bf16[768,768]{1,0:T(8,128)(2,1)} %copy-done.4, bf16[768,768]{1,0:T(8,128)(2,1)} %copy-done.3, bf16[768,768]{1,0:T(8,128)(2,1)} %copy-done.5), custom_call_target="tpu_custom_call" | custom-call | flops 2415919104 | bytes 11010048 | tf_op jit(solution)/shard_map/pallas_call | solution.py:416
  167.6 2.7 collective-permute-start.25
  173.2 1.7 fusion
  175.8 8.4 %collective-permute-done.25 = bf16[1,2,96,768]{3,2,1,0:T(8,128)(2,1)S(1)} collective-permute-done((bf16[1,2,96,768]{3,2,1,0:T(8,128)(2,1)S(1)}, bf16[1,2,96,768]{3,2,1,0:T(8,128)(2,1)S(1)}, u32[]{:S(2)}, u32[]{:S(2)}) %collective-permute-start.25) | collective-permute-done | bytes 294944 | tf_op jit(solution)/shard_map/ppermute | solution.py:459
  184.4 2.0 collective-permute-done.24
  186.6 2.1 collective-permute-start.31
  188.7 3.2 %shard_map.334 = (f32[256,768]{1,0:T(8,128)}, f32[40,768]{1,0:T(8,128)}) custom-call(f32[256,768]{1,0:T(8,128)} %get-tuple-element.138.grad_one_ref, f32[256,768]{1,0:T(8,128)} %get-tuple-element.155.own_ref, bf16[2,256,768]{2,1,0:T(8,128)(2,1)} %copy-done.11, bf16[256,768]{1,0:T(8,128)(2,1)} %collective-permute-done.23.far_ref, bf16[256,768]{1,0:T(8,128)(2,1)} %x_ref.5, ...), custom_call_target="tpu_custom_call" | custom-call | bytes 4068356 | tf_op jit(solution)/shard_map/pallas_call | solution.py:416
  191.9 8.4 %collective-permute-done.32 = bf16[1,2,96,768]{3,2,1,0:T(8,128)(2,1)S(1)} collective-permute-done((bf16[1,2,96,768]{3,2,1,0:T(8,128)(2,1)S(1)}, bf16[1,2,96,768]{3,2,1,0:T(8,128)(2,1)S(1)}, u32[]{:S(2)}, u32[]{:S(2)}) %collective-permute-start.32) | collective-permute-done | bytes 294944 | tf_op jit(solution)/shard_map/ppermute | solution.py:470
  201.9 12.5 %collective-permute-done.36 = bf16[2,2,96,768]{3,2,1,0:T(8,128)(2,1)S(1)} collective-permute-done((bf16[2,2,96,768]{3,2,1,0:T(8,128)(2,1)S(1)}, bf16[2,2,96,768]{3,2,1,0:T(8,128)(2,1)S(1)}, u32[]{:S(2)}, u32[]{:S(2)}) %collective-permute-start.36) | collective-permute-done | bytes 589856 | tf_op jit(solution)/shard_map/ppermute | solution.py:470
  217.2 1.7 collective-permute-start.34
  220.3 3.2 %collective-permute-done.35 = bf16[1,4,24,768]{3,2,1,0:T(8,128)(2,1)S(1)} collective-permute-done((bf16[1,4,24,768]{3,2,1,0:T(8,128)(2,1)S(1)}, bf16[1,4,24,768]{3,2,1,0:T(8,128)(2,1)S(1)}, u32[]{:S(2)}, u32[]{:S(2)}) %collective-permute-start.35) | collective-permute-done | bytes 147488 | tf_op jit(solution)/shard_map/ppermute | solution.py:459
  225.0 3.8 %collective-permute-done.34 = bf16[2,4,24,768]{3,2,1,0:T(8,128)(2,1)S(1)} collective-permute-done((bf16[2,4,24,768]{3,2,1,0:T(8,128)(2,1)S(1)}, bf16[2,4,24,768]{3,2,1,0:T(8,128)(2,1)S(1)}, u32[]{:S(2)}, u32[]{:S(2)}) %collective-permute-start.34) | collective-permute-done | bytes 294944 | tf_op jit(solution)/shard_map/ppermute | solution.py:459
  229.0 11.3 %collective-permute-done.40.high_ref = bf16[4,2,96,768]{3,2,1,0:T(8,128)(2,1)S(1)} collective-permute-done((bf16[4,2,96,768]{3,2,1,0:T(8,128)(2,1)S(1)}, bf16[4,2,96,768]{3,2,1,0:T(8,128)(2,1)S(1)}, u32[]{:S(2)}, u32[]{:S(2)}) %collective-permute-start.40) | collective-permute-done | bytes 1179680 | tf_op jit(solution)/shard_map/ppermute | solution.py:470
  242.4 3.8 %collective-permute-start.42 = (bf16[1,4,24,768]{3,2,1,0:T(8,128)(2,1)S(1)}, bf16[1,4,24,768]{3,2,1,0:T(8,128)(2,1)S(1)}, u32[]{:S(2)}, u32[]{:S(2)}) collective-permute-start(bf16[1,4,24,768]{3,2,1,0:T(8,128)(2,1)S(1)} %add_convert_fusion.10), channel_id=1, source_target_pairs={{0,16},{4,20},{8,24},{12,28},{16,0},{20,4},{24,8},{28,12},{1,17},{... | collective-permute-start | bytes 442376 | tf_op jit(solution)/shard_map/ppermute | solution.py:470
  246.2 3.4 %collective-permute-done.43 = bf16[2,4,24,768]{3,2,1,0:T(8,128)(2,1)S(1)} collective-permute-done((bf16[2,4,24,768]{3,2,1,0:T(8,128)(2,1)S(1)}, bf16[2,4,24,768]{3,2,1,0:T(8,128)(2,1)S(1)}, u32[]{:S(2)}, u32[]{:S(2)}) %collective-permute-start.43) | collective-permute-done | bytes 294944 | tf_op jit(solution)/shard_map/ppermute | solution.py:470
  249.7 2.1 collective-permute-start.46
  251.8 2.1 collective-permute-start.45
  256.2 5.2 %collective-permute-done.41 = f32[40,768]{1,0:T(8,128)} collective-permute-done((f32[40,768]{1,0:T(8,128)S(1)}, f32[40,768]{1,0:T(8,128)}, u32[]{:S(2)}, u32[]{:S(2)}) %collective-permute-start.41) | collective-permute-done | bytes 122912 | tf_op jit(solution)/shard_map/ppermute | solution.py:482
  262.3 2.6 collective-permute-start.44
  266.8 1.9 fusion.4
  268.7 4.1 %shard_map.337 = (f32[768,768]{1,0:T(8,128)}, f32[768,768]{1,0:T(8,128)}) custom-call(bf16[4,2,96,768]{3,2,1,0:T(8,128)(2,1)} %copy-done.6, bf16[4,2,96,768]{3,2,1,0:T(8,128)(2,1)} %copy-done.13, s32[1]{0:T(128)} %bitcast.10.turn_ref), custom_call_target="tpu_custom_call" | custom-call | bytes 7077892 | tf_op jit(solution)/shard_map/pallas_call | solution.py:416
  272.8 2.8 shard_map.335
  278.9 2.8 shard_map.336
  (179 shorter events, 42.0 us)
Async XLA Ops:
  2.6 12.3 %collective-permute-start.1 = (bf16[256,768]{1,0:T(8,128)(2,1)}, bf16[256,768]{1,0:T(8,128)(2,1)S(1)}, u32[]{:S(2)}, u32[]{:S(2)}) collective-permute-start(bf16[256,768]{1,0:T(8,128)(2,1)} %shard_map.323.n0), channel_id=1, source_target_pairs={{0,2},{2,0},{1,3},{3,1},{4,6},{6,4},{5,7},{7,5},{8,10},{10,8},{9,1... | collective-permute-start | bytes 1179656 | tf_op jit(solution)/shard_map/ppermute | solution.py:441
  5.5 12.6 %collective-permute-start = (bf16[256,768]{1,0:T(8,128)(2,1)}, bf16[256,768]{1,0:T(8,128)(2,1)S(1)}, u32[]{:S(2)}, u32[]{:S(2)}) collective-permute-start(bf16[256,768]{1,0:T(8,128)(2,1)} %shard_map.323.n0), channel_id=1, source_target_pairs={{0,1},{1,0},{2,3},{3,2},{4,5},{5,4},{6,7},{7,6},{8,9},{9,8},{10,11... | collective-permute-start | bytes 1179656 | tf_op jit(solution)/shard_map/ppermute | solution.py:437
  14.9 3.3 %collective-permute-start.2 = (bf16[256,768]{1,0:T(8,128)(2,1)S(1)}, bf16[256,768]{1,0:T(8,128)(2,1)}, u32[]{:S(2)}, u32[]{:S(2)}) collective-permute-start(bf16[256,768]{1,0:T(8,128)(2,1)S(1)} %collective-permute-done.1.n2), channel_id=1, source_target_pairs={{0,1},{1,0},{2,3},{3,2},{4,5},{5,4},{6,7},{7,6},{8,9},{9,8},{10,11... | collective-permute-start | bytes 1179656 | tf_op jit(solution)/shard_map/ppermute | solution.py:437
  16.3 28.3 %collective-permute-start.6 = (bf16[768,768]{1,0:T(8,128)(2,1)S(1)}, bf16[768,768]{1,0:T(8,128)(2,1)S(1)}, u32[]{:S(2)}, u32[]{:S(2)}) collective-permute-start(bf16[768,768]{1,0:T(8,128)(2,1)S(1)} %pad_maximum_fusion.w0), channel_id=1, source_target_pairs={{0,2},{2,0},{1,3},{3,1},{4,6},{6,4},{5,7},{7,5},{8,10},{10,8},{9,1... | collective-permute-start | bytes 3538952 | tf_op jit(solution)/shard_map/ppermute | solution.py:441
  27.9 2.9 %collective-permute-start.3 = (bf16[2,256,768]{2,1,0:T(8,128)(2,1)}, bf16[2,256,768]{2,1,0:T(8,128)(2,1)S(1)}, u32[]{:S(2)}, u32[]{:S(2)}) collective-permute-start(bf16[2,256,768]{2,1,0:T(8,128)(2,1)} %get-tuple-element.112), channel_id=1, source_target_pairs={{0,1},{1,0},{2,3},{3,2},{4,5},{5,4},{6,7},{7,6},{8,9},{9,8},{10,11... | collective-permute-start | bytes 2359304 | tf_op jit(solution)/shard_map/ppermute | solution.py:437
  27.9 18.5 %collective-permute-start.5 = (bf16[768,768]{1,0:T(8,128)(2,1)S(1)}, bf16[768,768]{1,0:T(8,128)(2,1)S(1)}, u32[]{:S(2)}, u32[]{:S(2)}) collective-permute-start(bf16[768,768]{1,0:T(8,128)(2,1)S(1)} %pad_maximum_fusion.w0), channel_id=1, source_target_pairs={{0,1},{1,0},{2,3},{3,2},{4,5},{5,4},{6,7},{7,6},{8,9},{9,8},{10,11... | collective-permute-start | bytes 3538952 | tf_op jit(solution)/shard_map/ppermute | solution.py:437
  44.6 2.8 %collective-permute-start.7 = (bf16[768,768]{1,0:T(8,128)(2,1)S(1)}, bf16[768,768]{1,0:T(8,128)(2,1)S(1)}, u32[]{:S(2)}, u32[]{:S(2)}) collective-permute-start(bf16[768,768]{1,0:T(8,128)(2,1)S(1)} %collective-permute-done.6.w2), channel_id=1, source_target_pairs={{0,1},{1,0},{2,3},{3,2},{4,5},{5,4},{6,7},{7,6},{8,9},{9,8},{10,11... | collective-permute-start | bytes 3538952 | tf_op jit(solution)/shard_map/ppermute | solution.py:437
  44.6 11.5 %collective-permute-start.4 = (bf16[256,768]{1,0:T(8,128)(2,1)S(1)}, bf16[256,768]{1,0:T(8,128)(2,1)S(1)}, u32[]{:S(2)}, u32[]{:S(2)}) collective-permute-start(bf16[256,768]{1,0:T(8,128)(2,1)S(1)} %fusion.7), channel_id=1, source_target_pairs={{0,2},{2,0},{1,3},{3,1},{4,6},{6,4},{5,7},{7,5},{8,10},{10,8},{9,1... | collective-permute-start | bytes 1179656 | tf_op jit(solution)/shard_map/ppermute | solution.py:441
  56.2 14.2 %collective-permute-start.11 = (bf16[256,768]{1,0:T(8,128)(2,1)S(1)}, bf16[256,768]{1,0:T(8,128)(2,1)S(1)}, u32[]{:S(2)}, u32[]{:S(2)}) collective-permute-start(bf16[256,768]{1,0:T(8,128)(2,1)S(1)} %copy-done.24), channel_id=1, source_target_pairs={{0,2},{2,0},{1,3},{3,1},{4,6},{6,4},{5,7},{7,5},{8,10},{10,8},{9,1... | collective-permute-start | bytes 1179656 | tf_op jit(solution)/shard_map/ppermute | solution.py:441
  57.9 13.5 %collective-permute-start.10 = (bf16[256,768]{1,0:T(8,128)(2,1)S(1)}, bf16[256,768]{1,0:T(8,128)(2,1)S(1)}, u32[]{:S(2)}, u32[]{:S(2)}) collective-permute-start(bf16[256,768]{1,0:T(8,128)(2,1)S(1)} %copy-done.24), channel_id=1, source_target_pairs={{0,1},{1,0},{2,3},{3,2},{4,5},{5,4},{6,7},{7,6},{8,9},{9,8},{10,11... | collective-permute-start | bytes 1179656 | tf_op jit(solution)/shard_map/ppermute | solution.py:437
  70.4 1.9 collective-permute-start.12
  71.0 11.3 %collective-permute-start.9 = (bf16[256,768]{1,0:T(8,128)(2,1)}, bf16[256,768]{1,0:T(8,128)(2,1)S(1)}, u32[]{:S(2)}, u32[]{:S(2)}) collective-permute-start(bf16[256,768]{1,0:T(8,128)(2,1)} %get-tuple-element.120.g0), channel_id=1, source_target_pairs={{0,2},{2,0},{1,3},{3,1},{4,6},{6,4},{5,7},{7,5},{8,10},{10,8},{9,1... | collective-permute-start | bytes 1179656 | tf_op jit(solution)/shard_map/ppermute | solution.py:441
  71.3 11.0 %collective-permute-start.8 = (bf16[256,768]{1,0:T(8,128)(2,1)}, bf16[256,768]{1,0:T(8,128)(2,1)S(1)}, u32[]{:S(2)}, u32[]{:S(2)}) collective-permute-start(bf16[256,768]{1,0:T(8,128)(2,1)} %get-tuple-element.120.g0), channel_id=1, source_target_pairs={{0,1},{1,0},{2,3},{3,2},{4,5},{5,4},{6,7},{7,6},{8,9},{9,8},{10,11... | collective-permute-start | bytes 1179656 | tf_op jit(solution)/shard_map/ppermute | solution.py:437
  82.3 1.7 collective-permute-start.13
  92.8 2.5 collective-permute-start.14
  96.8 11.2 %collective-permute-start.15 = (bf16[256,768]{1,0:T(8,128)(2,1)S(1)}, bf16[256,768]{1,0:T(8,128)(2,1)S(1)}, u32[]{:S(2)}, u32[]{:S(2)}) collective-permute-start(bf16[256,768]{1,0:T(8,128)(2,1)S(1)} %fusion.6), channel_id=1, source_target_pairs={{0,2},{2,0},{1,3},{3,1},{4,6},{6,4},{5,7},{7,5},{8,10},{10,8},{9,1... | collective-permute-start | bytes 1179656 | tf_op jit(solution)/shard_map/ppermute | solution.py:441
  105.6 33.1 %collective-permute-start.18 = (bf16[4,2,96,768]{3,2,1,0:T(8,128)(2,1)}, bf16[4,2,96,768]{3,2,1,0:T(8,128)(2,1)S(1)}, u32[]{:S(2)}, u32[]{:S(2)}) collective-permute-start(bf16[4,2,96,768]{3,2,1,0:T(8,128)(2,1)} %get-tuple-element.132), channel_id=1, source_target_pairs={{0,4},{4,0},{8,12},{12,8},{16,20},{20,16},{24,28},{28,24},{1,5},{5... | collective-permute-start | bytes 3538952 | tf_op jit(solution)/shard_map/ppermute | solution.py:459
  128.0 10.7 %collective-permute-start.17 = (bf16[256,768]{1,0:T(8,128)(2,1)}, bf16[256,768]{1,0:T(8,128)(2,1)}, u32[]{:S(2)}, u32[]{:S(2)}) collective-permute-start(bf16[256,768]{1,0:T(8,128)(2,1)} %get-tuple-element.139.u0), channel_id=1, source_target_pairs={{0,2},{2,0},{1,3},{3,1},{4,6},{6,4},{5,7},{7,5},{8,10},{10,8},{9,1... | collective-permute-start | bytes 1179656 | tf_op jit(solution)/shard_map/ppermute | solution.py:441
  139.1 4.8 %collective-permute-start.19 = (bf16[2,8,4,24,768]{4,3,2,1,0:T(8,128)(2,1)}, bf16[2,8,4,24,768]{4,3,2,1,0:T(8,128)(2,1)S(1)}, u32[]{:S(2)}, u32[]{:S(2)}) collective-permute-start(bf16[2,8,4,24,768]{4,3,2,1,0:T(8,128)(2,1)} %get-tuple-element.149), channel_id=1, source_target_pairs={{0,1},{1,0},{2,3},{3,2},{4,5},{5,4},{6,7},{7,6},{8,9},{9,8},{10,11... | collective-permute-start | bytes 7077896 | tf_op jit(solution)/shard_map/ppermute | solution.py:437
  139.8 5.3 %collective-permute-start.16 = (bf16[256,768]{1,0:T(8,128)(2,1)S(1)}, bf16[256,768]{1,0:T(8,128)(2,1)S(1)}, u32[]{:S(2)}, u32[]{:S(2)}) collective-permute-start(bf16[256,768]{1,0:T(8,128)(2,1)S(1)} %copy-done.35), channel_id=1, source_target_pairs={{0,1},{1,0},{2,3},{3,2},{4,5},{5,4},{6,7},{7,6},{8,9},{9,8},{10,11... | collective-permute-start | bytes 1179656 | tf_op jit(solution)/shard_map/ppermute | solution.py:437
  139.8 6.1 %collective-permute-start.20 = (bf16[256,768]{1,0:T(8,128)(2,1)}, bf16[256,768]{1,0:T(8,128)(2,1)S(1)}, u32[]{:S(2)}, u32[]{:S(2)}) collective-permute-start(bf16[256,768]{1,0:T(8,128)(2,1)} %collective-permute-done.17.u2), channel_id=1, source_target_pairs={{0,1},{1,0},{2,3},{3,2},{4,5},{5,4},{6,7},{7,6},{8,9},{9,8},{10,11... | collective-permute-start | bytes 1179656 | tf_op jit(solution)/shard_map/ppermute | solution.py:437
  140.3 27.2 %collective-permute-start.21 = (bf16[2,2,96,768]{3,2,1,0:T(8,128)(2,1)S(1)}, bf16[2,2,96,768]{3,2,1,0:T(8,128)(2,1)S(1)}, u32[]{:S(2)}, u32[]{:S(2)}) collective-permute-start(bf16[2,2,96,768]{3,2,1,0:T(8,128)(2,1)S(1)} %get-tuple-element.207), channel_id=1, source_target_pairs={{0,8},{4,12},{8,0},{12,4},{16,24},{20,28},{24,16},{28,20},{1,9},{5... | collective-permute-start | bytes 1769480 | tf_op jit(solution)/shard_map/ppermute | solution.py:459
  144.2 28.9 %collective-permute-start.26 = (bf16[8,4,24,768]{3,2,1,0:T(8,128)(2,1)S(1)}, bf16[8,4,24,768]{3,2,1,0:T(8,128)(2,1)}, u32[]{:S(2)}, u32[]{:S(2)}) collective-permute-start(bf16[8,4,24,768]{3,2,1,0:T(8,128)(2,1)S(1)} %fusion.1), channel_id=1, source_target_pairs={{0,2},{2,0},{1,3},{3,1},{4,6},{6,4},{5,7},{7,5},{8,10},{10,8},{9,1... | collective-permute-start | bytes 3538952 | tf_op jit(solution)/shard_map/ppermute | solution.py:441
  167.5 4.1 %collective-permute-start.22 = (bf16[2,256,768]{2,1,0:T(8,128)(2,1)}, bf16[2,256,768]{2,1,0:T(8,128)(2,1)S(1)}, u32[]{:S(2)}, u32[]{:S(2)}) collective-permute-start(bf16[2,256,768]{2,1,0:T(8,128)(2,1)} %get-tuple-element.162), channel_id=1, source_target_pairs={{0,1},{1,0},{2,3},{3,2},{4,5},{5,4},{6,7},{7,6},{8,9},{9,8},{10,11... | collective-permute-start | bytes 2359304 | tf_op jit(solution)/shard_map/ppermute | solution.py:437
  167.6 16.6 %collective-permute-start.25 = (bf16[1,2,96,768]{3,2,1,0:T(8,128)(2,1)S(1)}, bf16[1,2,96,768]{3,2,1,0:T(8,128)(2,1)S(1)}, u32[]{:S(2)}, u32[]{:S(2)}) collective-permute-start(bf16[1,2,96,768]{3,2,1,0:T(8,128)(2,1)S(1)} %add_convert_fusion.9), channel_id=1, source_target_pairs={{0,16},{4,20},{8,24},{12,28},{16,0},{20,4},{24,8},{28,12},{1,17},{... | collective-permute-start | bytes 884744 | tf_op jit(solution)/shard_map/ppermute | solution.py:459
  170.2 16.2 %collective-permute-start.24 = (bf16[4,4,24,768]{3,2,1,0:T(8,128)(2,1)S(1)}, bf16[4,4,24,768]{3,2,1,0:T(8,128)(2,1)S(1)}, u32[]{:S(2)}, u32[]{:S(2)}) collective-permute-start(bf16[4,4,24,768]{3,2,1,0:T(8,128)(2,1)S(1)} %copy-done.31), channel_id=1, source_target_pairs={{0,4},{4,0},{8,12},{12,8},{16,20},{20,16},{24,28},{28,24},{1,5},{5... | collective-permute-start | bytes 1769480 | tf_op jit(solution)/shard_map/ppermute | solution.py:459
  171.7 17.0 %collective-permute-start.23 = (bf16[256,768]{1,0:T(8,128)(2,1)S(1)}, bf16[256,768]{1,0:T(8,128)(2,1)}, u32[]{:S(2)}, u32[]{:S(2)}) collective-permute-start(bf16[256,768]{1,0:T(8,128)(2,1)S(1)} %fusion.5), channel_id=1, source_target_pairs={{0,2},{2,0},{1,3},{3,1},{4,6},{6,4},{5,7},{7,5},{8,10},{10,8},{9,1... | collective-permute-start | bytes 1179656 | tf_op jit(solution)/shard_map/ppermute | solution.py:441
  175.0 25.7 %collective-permute-start.30 = (bf16[4,4,24,768]{3,2,1,0:T(8,128)(2,1)S(1)}, bf16[4,4,24,768]{3,2,1,0:T(8,128)(2,1)S(1)}, u32[]{:S(2)}, u32[]{:S(2)}) collective-permute-start(bf16[4,4,24,768]{3,2,1,0:T(8,128)(2,1)S(1)} %slice.162), channel_id=1, source_target_pairs={{0,4},{4,0},{8,12},{12,8},{16,20},{20,16},{24,28},{28,24},{1,5},{5... | collective-permute-start | bytes 1769480 | tf_op jit(solution)/shard_map/ppermute | solution.py:459
  184.3 16.0 %collective-permute-start.32 = (bf16[1,2,96,768]{3,2,1,0:T(8,128)(2,1)S(1)}, bf16[1,2,96,768]{3,2,1,0:T(8,128)(2,1)S(1)}, u32[]{:S(2)}, u32[]{:S(2)}) collective-permute-start(bf16[1,2,96,768]{3,2,1,0:T(8,128)(2,1)S(1)} %add_convert_fusion.7), channel_id=1, source_target_pairs={{0,16},{4,20},{8,24},{12,28},{16,0},{20,4},{24,8},{28,12},{1,17},{... | collective-permute-start | bytes 884744 | tf_op jit(solution)/shard_map/ppermute | solution.py:470
  186.6 14.0 %collective-permute-start.31 = (bf16[2,4,24,768]{3,2,1,0:T(8,128)(2,1)S(1)}, bf16[2,4,24,768]{3,2,1,0:T(8,128)(2,1)S(1)}, u32[]{:S(2)}, u32[]{:S(2)}) collective-permute-start(bf16[2,4,24,768]{3,2,1,0:T(8,128)(2,1)S(1)} %get-tuple-element.211), channel_id=1, source_target_pairs={{0,8},{4,12},{8,0},{12,4},{16,24},{20,28},{24,16},{28,20},{1,9},{5... | collective-permute-start | bytes 884744 | tf_op jit(solution)/shard_map/ppermute | solution.py:459
  200.4 14.0 %collective-permute-start.36 = (bf16[2,2,96,768]{3,2,1,0:T(8,128)(2,1)S(1)}, bf16[2,2,96,768]{3,2,1,0:T(8,128)(2,1)S(1)}, u32[]{:S(2)}, u32[]{:S(2)}) collective-permute-start(bf16[2,2,96,768]{3,2,1,0:T(8,128)(2,1)S(1)} %pad_maximum_fusion.2), channel_id=1, source_target_pairs={{0,8},{4,12},{8,0},{12,4},{16,24},{20,28},{24,16},{28,20},{1,9},{5... | collective-permute-start | bytes 1769480 | tf_op jit(solution)/shard_map/ppermute | solution.py:470
  200.5 1.4 collective-permute-start.29
  214.5 25.7 %collective-permute-start.40 = (bf16[4,2,96,768]{3,2,1,0:T(8,128)(2,1)S(1)}, bf16[4,2,96,768]{3,2,1,0:T(8,128)(2,1)S(1)}, u32[]{:S(2)}, u32[]{:S(2)}) collective-permute-start(bf16[4,2,96,768]{3,2,1,0:T(8,128)(2,1)S(1)} %pad_maximum_fusion.1.low_ref), channel_id=1, source_target_pairs={{0,4},{4,0},{8,12},{12,8},{16,20},{20,16},{24,28},{28,24},{1,5},{5... | collective-permute-start | bytes 3538952 | tf_op jit(solution)/shard_map/ppermute | solution.py:470
  216.0 7.6 %collective-permute-start.35 = (bf16[1,4,24,768]{3,2,1,0:T(8,128)(2,1)S(1)}, bf16[1,4,24,768]{3,2,1,0:T(8,128)(2,1)S(1)}, u32[]{:S(2)}, u32[]{:S(2)}) collective-permute-start(bf16[1,4,24,768]{3,2,1,0:T(8,128)(2,1)S(1)} %add_convert_fusion.15), channel_id=1, source_target_pairs={{0,16},{4,20},{8,24},{12,28},{16,0},{20,4},{24,8},{28,12},{1,17},{... | collective-permute-start | bytes 442376 | tf_op jit(solution)/shard_map/ppermute | solution.py:459
  217.2 11.6 %collective-permute-start.34 = (bf16[2,4,24,768]{3,2,1,0:T(8,128)(2,1)S(1)}, bf16[2,4,24,768]{3,2,1,0:T(8,128)(2,1)S(1)}, u32[]{:S(2)}, u32[]{:S(2)}) collective-permute-start(bf16[2,4,24,768]{3,2,1,0:T(8,128)(2,1)S(1)} %get-tuple-element.209), channel_id=1, source_target_pairs={{0,8},{4,12},{8,0},{12,4},{16,24},{20,28},{24,16},{28,20},{1,9},{5... | collective-permute-start | bytes 884744 | tf_op jit(solution)/shard_map/ppermute | solution.py:459
  219.0 35.0 %collective-permute-start.27 = (bf16[2,256,768]{2,1,0:T(8,128)(2,1)S(1)}, bf16[2,256,768]{2,1,0:T(8,128)(2,1)S(1)}, u32[]{:S(2)}, u32[]{:S(2)}) collective-permute-start(bf16[2,256,768]{2,1,0:T(8,128)(2,1)S(1)} %copy-done.30), channel_id=1, source_target_pairs={{0,1},{1,0},{2,3},{3,2},{4,5},{5,4},{6,7},{7,6},{8,9},{9,8},{10,11... | collective-permute-start | bytes 2359304 | tf_op jit(solution)/shard_map/ppermute | solution.py:437
  219.0 10.0 %collective-permute-start.33 = (f32[40,768]{1,0:T(8,128)S(1)}, f32[40,768]{1,0:T(8,128)S(1)}, u32[]{:S(2)}, u32[]{:S(2)}) collective-permute-start(f32[40,768]{1,0:T(8,128)S(1)} %add.146), channel_id=1, source_target_pairs={{0,2},{1,3},{2,0},{3,1},{4,6},{5,7},{6,4},{7,5},{8,10},{9,11},{10,... | collective-permute-start | bytes 368648 | tf_op jit(solution)/shard_map/ppermute | solution.py:482
  223.6 16.6 %collective-permute-start.39 = (bf16[1,4,24,768]{3,2,1,0:T(8,128)(2,1)S(1)}, bf16[1,4,24,768]{3,2,1,0:T(8,128)(2,1)S(1)}, u32[]{:S(2)}, u32[]{:S(2)}) collective-permute-start(bf16[1,4,24,768]{3,2,1,0:T(8,128)(2,1)S(1)} %add_convert_fusion.13), channel_id=1, source_target_pairs={{0,16},{4,20},{8,24},{12,28},{16,0},{20,4},{24,8},{28,12},{1,17},{... | collective-permute-start | bytes 442376 | tf_op jit(solution)/shard_map/ppermute | solution.py:470
  228.9 13.4 %collective-permute-start.38 = (bf16[1,4,24,768]{3,2,1,0:T(8,128)(2,1)S(1)}, bf16[1,4,24,768]{3,2,1,0:T(8,128)(2,1)S(1)}, u32[]{:S(2)}, u32[]{:S(2)}) collective-permute-start(bf16[1,4,24,768]{3,2,1,0:T(8,128)(2,1)S(1)} %add_convert_fusion.12), channel_id=1, source_target_pairs={{0,16},{4,20},{8,24},{12,28},{16,0},{20,4},{24,8},{28,12},{1,17},{... | collective-permute-start | bytes 442376 | tf_op jit(solution)/shard_map/ppermute | solution.py:459
  240.3 9.3 %collective-permute-start.43 = (bf16[2,4,24,768]{3,2,1,0:T(8,128)(2,1)S(1)}, bf16[2,4,24,768]{3,2,1,0:T(8,128)(2,1)S(1)}, u32[]{:S(2)}, u32[]{:S(2)}) collective-permute-start(bf16[2,4,24,768]{3,2,1,0:T(8,128)(2,1)S(1)} %pad_maximum_fusion.5), channel_id=1, source_target_pairs={{0,8},{4,12},{8,0},{12,4},{16,24},{20,28},{24,16},{28,20},{1,9},{5... | collective-permute-start | bytes 884744 | tf_op jit(solution)/shard_map/ppermute | solution.py:470
  240.9 5.3 %collective-permute-start.37 = (f32[40,768]{1,0:T(8,128)S(1)}, f32[40,768]{1,0:T(8,128)S(1)}, u32[]{:S(2)}, u32[]{:S(2)}) collective-permute-start(f32[40,768]{1,0:T(8,128)S(1)} %add.151), channel_id=1, source_target_pairs={{0,4},{4,0},{8,12},{12,8},{16,20},{20,16},{24,28},{28,24},{1,5},{5... | collective-permute-start | bytes 368648 | tf_op jit(solution)/shard_map/ppermute | solution.py:482
  242.4 9.4 %collective-permute-start.42 = (bf16[1,4,24,768]{3,2,1,0:T(8,128)(2,1)S(1)}, bf16[1,4,24,768]{3,2,1,0:T(8,128)(2,1)S(1)}, u32[]{:S(2)}, u32[]{:S(2)}) collective-permute-start(bf16[1,4,24,768]{3,2,1,0:T(8,128)(2,1)S(1)} %add_convert_fusion.10), channel_id=1, source_target_pairs={{0,16},{4,20},{8,24},{12,28},{16,0},{20,4},{24,8},{28,12},{1,17},{... | collective-permute-start | bytes 442376 | tf_op jit(solution)/shard_map/ppermute | solution.py:470
  249.7 15.3 %collective-permute-start.46 = (bf16[4,4,24,768]{3,2,1,0:T(8,128)(2,1)S(1)}, bf16[4,4,24,768]{3,2,1,0:T(8,128)(2,1)S(1)}, u32[]{:S(2)}, u32[]{:S(2)}) collective-permute-start(bf16[4,4,24,768]{3,2,1,0:T(8,128)(2,1)S(1)} %pad_maximum_fusion.3.low_ref), channel_id=1, source_target_pairs={{0,4},{4,0},{8,12},{12,8},{16,20},{20,16},{24,28},{28,24},{1,5},{5... | collective-permute-start | bytes 1769480 | tf_op jit(solution)/shard_map/ppermute | solution.py:470
  251.8 13.2 %collective-permute-start.45 = (bf16[2,4,24,768]{3,2,1,0:T(8,128)(2,1)S(1)}, bf16[2,4,24,768]{3,2,1,0:T(8,128)(2,1)}, u32[]{:S(2)}, u32[]{:S(2)}) collective-permute-start(bf16[2,4,24,768]{3,2,1,0:T(8,128)(2,1)S(1)} %pad_maximum_fusion.6), channel_id=1, source_target_pairs={{0,8},{4,12},{8,0},{12,4},{16,24},{20,28},{24,16},{28,20},{1,9},{5... | collective-permute-start | bytes 884744 | tf_op jit(solution)/shard_map/ppermute | solution.py:470
  254.9 11.8 %collective-permute-start.28 = (bf16[256,768]{1,0:T(8,128)(2,1)}, bf16[256,768]{1,0:T(8,128)(2,1)}, u32[]{:S(2)}, u32[]{:S(2)}) collective-permute-start(bf16[256,768]{1,0:T(8,128)(2,1)} %fusion.2), channel_id=1, source_target_pairs={{0,2},{2,0},{1,3},{3,1},{4,6},{6,4},{5,7},{7,5},{8,10},{10,8},{9,1... | collective-permute-start | bytes 1179656 | tf_op jit(solution)/shard_map/ppermute | solution.py:441
  256.2 5.2 %collective-permute-start.41 = (f32[40,768]{1,0:T(8,128)S(1)}, f32[40,768]{1,0:T(8,128)}, u32[]{:S(2)}, u32[]{:S(2)}) collective-permute-start(f32[40,768]{1,0:T(8,128)S(1)} %add.154), channel_id=1, source_target_pairs={{0,8},{4,12},{8,0},{12,4},{16,24},{20,28},{24,16},{28,20},{1,9},{5... | collective-permute-start | bytes 368648 | tf_op jit(solution)/shard_map/ppermute | solution.py:482
  262.3 13.3 %collective-permute-start.44 = (f32[40,768]{1,0:T(8,128)S(1)}, f32[40,768]{1,0:T(8,128)S(1)}, u32[]{:S(2)}, u32[]{:S(2)}) collective-permute-start(f32[40,768]{1,0:T(8,128)S(1)} %add.155), channel_id=1, source_target_pairs={{0,16},{4,20},{8,24},{12,28},{16,0},{20,4},{24,8},{28,12},{1,17},{... | collective-permute-start | bytes 368648 | tf_op jit(solution)/shard_map/ppermute | solution.py:482
  266.2 11.9 %collective-permute-start.47 = (bf16[4,4,24,768]{3,2,1,0:T(8,128)(2,1)S(1)}, bf16[4,4,24,768]{3,2,1,0:T(8,128)(2,1)S(1)}, u32[]{:S(2)}, u32[]{:S(2)}) collective-permute-start(bf16[4,4,24,768]{3,2,1,0:T(8,128)(2,1)S(1)} %pad_maximum_fusion.4.low_ref), channel_id=1, source_target_pairs={{0,4},{4,0},{8,12},{12,8},{16,20},{20,16},{24,28},{28,24},{1,5},{5... | collective-permute-start | bytes 1769480 | tf_op jit(solution)/shard_map/ppermute | solution.py:470
  (41 other events, 285.0 us)
